TPU v7x, 8 devices: a whole 2x2x1 slice. The times are simulated.
8 devices in a mesh: tp: 2 (over z, y), dp: 4 (over x, core).
Axes of the slice: x: 2, y: 2, z: 1, core: 2. Of those that a mesh axis runs over, the one named last changes fastest.
Arguments:
- x_in: bfloat16 [128, 3584], P(('dp', 'tp'))
- w_gate: bfloat16 [3584, 18944], P('dp', 'tp')
- w_up: bfloat16 [3584, 18944], P('dp', 'tp')
- w_down: bfloat16 [18944, 3584], P('tp', 'dp')
- grad_y: bfloat16 [128, 3584], P(('dp', 'tp'))
Outputs:
- output 1: bfloat16 [128, 3584], P(('dp', 'tp'))
- output 2: bfloat16 [128, 3584], P(('dp', 'tp'))
- output 3: float32 [3584, 18944], P('dp', 'tp')
- output 4: float32 [3584, 18944], P('dp', 'tp')
- output 5: float32 [18944, 3584], P('tp', 'dp')
All inputs are finite; a program needn't handle non-finite values.
Results may differ from a plain program's by a relative error of at most 0.00101.
Values are sent between devices in bfloat16 or wider.
A program may use at most 1 GiB of HBM per device.

v0:
```python
import jax
import jax.numpy as jnp
from jax import lax
from jax.sharding import PartitionSpec as P


def solution(mesh):
    dp_size = mesh.shape["dp"]
    tp_size = mesh.shape["tp"]

    def spread_cols(rows_loc):
        tok_dev = rows_loc.shape[0]
        cols_mine = lax.all_to_all(rows_loc, "dp", 1, 0, tiled=True)
        col_width = cols_mine.shape[1]
        cols_mine = cols_mine.reshape(dp_size, tok_dev, col_width)
        gathered = lax.all_gather(cols_mine, "tp", axis=1)
        return cols_mine, gathered.reshape(dp_size * tp_size * tok_dev, col_width)

    def collect_rows(col_part, resid):
        tok_dev = resid.shape[1]
        col_width = col_part.shape[1]
        summed = lax.psum_scatter(col_part.reshape(dp_size, tp_size, tok_dev, col_width), "tp", scatter_dimension=1, tiled=True)
        summed = summed.reshape(dp_size, tok_dev, col_width) + resid.astype(jnp.float32)
        out_rows = lax.all_to_all(summed.astype(jnp.bfloat16), "dp", 0, 2, tiled=True)
        return out_rows.reshape(tok_dev, dp_size * col_width)

    def local_step(x_loc, wg_loc, wu_loc, wd_loc, gy_loc):
        x_mine, x_cols = spread_cols(x_loc)
        gate_pre = lax.psum_scatter(jnp.dot(x_cols, wg_loc, preferred_element_type=jnp.float32), "dp", scatter_dimension=0, tiled=True)
        up_pre = lax.psum_scatter(jnp.dot(x_cols, wu_loc, preferred_element_type=jnp.float32), "dp", scatter_dimension=0, tiled=True)
        sig_gate = jax.nn.sigmoid(gate_pre)
        silu_gate = gate_pre * sig_gate
        hidden = (silu_gate * up_pre).astype(jnp.bfloat16)
        hidden_all = lax.all_gather(hidden, "dp", axis=0, tiled=True)
        y_rows = collect_rows(jnp.dot(hidden_all, wd_loc, preferred_element_type=jnp.float32), x_mine)

        gy_mine, gy_cols = spread_cols(gy_loc)
        grad_h = lax.psum_scatter(jnp.einsum("nd,fd->nf", gy_cols, wd_loc, preferred_element_type=jnp.float32), "dp", scatter_dimension=0, tiled=True)
        grad_wd = jnp.einsum("nf,nd->fd", hidden_all, gy_cols, preferred_element_type=jnp.float32)
        silu_deriv = sig_gate * (1.0 + gate_pre * (1.0 - sig_gate))
        grad_gate = (grad_h * up_pre * silu_deriv).astype(jnp.bfloat16)
        grad_up = (grad_h * silu_gate).astype(jnp.bfloat16)
        gate_all = lax.all_gather(grad_gate, "dp", axis=0, tiled=True)
        up_all = lax.all_gather(grad_up, "dp", axis=0, tiled=True)
        grad_wg = jnp.einsum("nd,nf->df", x_cols, gate_all, preferred_element_type=jnp.float32)
        grad_wu = jnp.einsum("nd,nf->df", x_cols, up_all, preferred_element_type=jnp.float32)
        gx_part = (jnp.einsum("nf,df->nd", gate_all, wg_loc, preferred_element_type=jnp.float32)
                   + jnp.einsum("nf,df->nd", up_all, wu_loc, preferred_element_type=jnp.float32))
        gx_rows = collect_rows(gx_part, gy_mine)
        return y_rows, gx_rows, grad_wg, grad_wu, grad_wd

    row_spec = P(("dp", "tp"), None)
    up_spec = P("dp", "tp")
    down_spec = P("tp", "dp")
    return jax.shard_map(local_step, mesh=mesh,
                         in_specs=(row_spec, up_spec, up_spec, down_spec, row_spec),
                         out_specs=(row_spec, row_spec, up_spec, up_spec, down_spec),
                         check_vma=False)
```

profile of v0, /device:TPU:0, one launch (start us, length us, event | category | flops | bytes accessed | tf_op | source)
XLA Modules:
  0.0 390.7 jit_solution(2716063004688807235)
XLA Ops:
  8.1 8.8 %all_to_all.62 = bf16[16,4,896]{2,0,1:T(8,128)(2,1)S(1)} all-to-all(bf16[16,4,896]{2,0,1:T(8,128)(2,1)S(1)} %bitcast.81), channel_id=1, replica_groups=mesh['tp'=2,'dp'=4] {'dp'}, dimensions={1} | all-to-all | bytes 229376 | tf_op jit(solution)/shard_map/all_to_all | solution.py:13
  17.0 5.5 %all-gather = bf16[4,32,896]{2,0,1:T(4,128)(2,1)S(1)} all-gather(bf16[4,16,896]{2,0,1:T(4,128)(2,1)S(1)} %copy.29), channel_id=2, replica_groups=mesh['tp'=2,'dp'=4] {'tp'}, dimensions={1}, use_global_device_ids=true | all-gather | bytes 344064 | tf_op jit(solution)/shard_map/all_gather | solution.py:16
  22.5 10.8 %fusion.5 = f32[128,9472]{1,0:T(8,128)} fusion(bf16[128,896]{1,0:T(8,128)(2,1)S(1)} %bitcast.67, bf16[896,9472]{1,0:T(8,128)(2,1)} %param.6), kind=kOutput, calls=%fused_computation.16 | convolution fusion | flops 2172649472 | bytes 22052864 | tf_op jit(solution)/shard_map/dot_general | solution.py:29
  33.3 10.8 %fusion.6 = f32[128,9472]{1,0:T(8,128)} fusion(bf16[128,896]{1,0:T(8,128)(2,1)S(1)} %bitcast.68, bf16[896,9472]{1,0:T(8,128)(2,1)} %param.7), kind=kOutput, calls=%fused_computation.17 | convolution fusion | flops 2172649472 | bytes 22052864 | tf_op jit(solution)/shard_map/dot_general | solution.py:30
  45.0 8.4 %all_to_all.63 = bf16[16,4,896]{2,0,1:T(8,128)(2,1)S(1)} all-to-all(bf16[16,4,896]{2,0,1:T(8,128)(2,1)S(1)} %bitcast.82), channel_id=1, replica_groups=mesh['tp'=2,'dp'=4] {'dp'}, dimensions={1} | all-to-all | bytes 229376 | tf_op jit(solution)/shard_map/all_to_all | solution.py:13
  54.1 5.4 %all-gather.1 = bf16[4,32,896]{2,0,1:T(4,128)(2,1)S(1)} all-gather(bf16[4,16,896]{2,0,1:T(4,128)(2,1)S(1)} %copy.33), channel_id=3, replica_groups=mesh['tp'=2,'dp'=4] {'tp'}, dimensions={1}, use_global_device_ids=true | all-gather | bytes 344064 | tf_op jit(solution)/shard_map/all_gather | solution.py:16
  59.5 12.7 %fusion.8 = f32[128,9472]{1,0:T(8,128)} fusion(bf16[128,896]{1,0:T(8,128)(2,1)S(1)} %bitcast.71, bf16[9472,896]{1,0:T(8,128)(2,1)} %param.8), kind=kOutput, calls=%fused_computation.19 | convolution fusion | flops 2172649472 | bytes 22052864 | tf_op jit(solution)/shard_map/nd,fd->nf/dot_general | solution.py:38
  72.3 4.8 %reduce-scatter.6.cloned.1.call-done = f32[32,9472]{1,0:T(8,128)} async-done(((f32[128,9472]{1,0:T(8,128)}), f32[32,9472]{1,0:T(8,128)}) %reduce-scatter.6.cloned.1.call-update) | async-done | bytes 1212432 | tf_op jit(solution)/shard_map/reduce_scatter | solution.py:29
  77.1 45.5 %reduce-scatter.8.cloned.1.call-done = f32[32,9472]{1,0:T(8,128)} async-done(((f32[128,9472]{1,0:T(8,128)}), f32[32,9472]{1,0:T(8,128)}) %reduce-scatter.8.cloned.1.call-update) | async-done | bytes 1212432 | tf_op jit(solution)/shard_map/reduce_scatter | solution.py:30
  122.6 45.5 %reduce-scatter.10.cloned.1.call-done = f32[32,9472]{1,0:T(8,128)} async-done(((f32[128,9472]{1,0:T(8,128)}), f32[32,9472]{1,0:T(8,128)}) %reduce-scatter.10.cloned.1.call-update) | async-done | bytes 1212432 | tf_op jit(solution)/shard_map/reduce_scatter | solution.py:38
  168.0 3.7 multiply_convert_fusion
  173.8 19.4 %all-gather.8.cloned.1.call-done = bf16[128,9472]{1,0:T(8,128)(2,1)} async-done(((bf16[32,9472]{1,0:T(8,128)(2,1)}), bf16[128,9472]{1,0:T(8,128)(2,1)}) %all-gather.8.cloned.1.call-update) | async-done | bytes 2424848 | tf_op jit(solution)/shard_map/all_gather | solution.py:43
  193.2 11.8 %fusion.9 = f32[128,896]{1,0:T(8,128)S(1)} fusion(bf16[128,9472]{1,0:T(8,128)(2,1)} %all-gather.8.cloned.1.call-done, bf16[896,9472]{1,0:T(8,128)(2,1)} %param.6), kind=kOutput, calls=%fused_computation.20 | convolution fusion | flops 2172649472 | bytes 19857408 | tf_op jit(solution)/shard_map/nf,df->nd/dot_general | solution.py:47
  205.1 11.4 %all-gather.6.cloned.1.call-done = bf16[128,9472]{1,0:T(8,128)(2,1)} async-done(((bf16[32,9472]{1,0:T(8,128)(2,1)}), bf16[128,9472]{1,0:T(8,128)(2,1)}) %all-gather.6.cloned.1.call-update) | async-done | bytes 2424848 | tf_op jit(solution)/shard_map/all_gather | solution.py:34
  216.5 10.0 %fusion.7 = f32[128,896]{1,0:T(8,128)} fusion(bf16[128,9472]{1,0:T(8,128)(2,1)} %all-gather.6.cloned.1.call-done, bf16[9472,896]{1,0:T(8,128)(2,1)} %param.8), kind=kOutput, calls=%fused_computation.18 | convolution fusion | flops 2172649472 | bytes 19857408 | tf_op jit(solution)/shard_map/dot_general | solution.py:35
  226.5 13.3 %all-gather.10.cloned.1.call-done = bf16[128,9472]{1,0:T(8,128)(2,1)} async-done(((bf16[32,9472]{1,0:T(8,128)(2,1)}), bf16[128,9472]{1,0:T(8,128)(2,1)}) %all-gather.10.cloned.1.call-update) | async-done | bytes 2424848 | tf_op jit(solution)/shard_map/all_gather | solution.py:44
  239.8 12.8 %convolution_add_fusion = f32[128,896]{1,0:T(8,128)} fusion(f32[128,896]{1,0:T(8,128)S(1)} %fusion.9, bf16[128,9472]{1,0:T(8,128)(2,1)} %all-gather.10.cloned.1.call-done, bf16[896,9472]{1,0:T(8,128)(2,1)} %param.7), kind=kOutput, calls=%fused_computation.7 | convolution fusion | flops 2172764160 | bytes 20316160 | tf_op jit(solution)/shard_map/nf,df->nd/dot_general | solution.py:48
  252.6 14.5 %convolution_bitcast_fusion.1 = f32[896,9472]{0,1:T(8,128)} fusion(bf16[128,9472]{1,0:T(8,128)(2,1)S(1)} %copy-done.1, bf16[128,896]{1,0:T(8,128)(2,1)S(1)} %bitcast.69), kind=kOutput, calls=%fused_computation.1 | convolution fusion | flops 2172649472 | bytes 36601856 | tf_op jit(solution)/shard_map/nd,nf->df/dot_general | solution.py:45
  267.0 13.3 %convolution_bitcast_fusion = f32[896,9472]{0,1:T(8,128)} fusion(bf16[128,9472]{1,0:T(8,128)(2,1)S(1)} %copy-done.2, bf16[128,896]{1,0:T(8,128)(2,1)S(1)} %bitcast.70), kind=kOutput, calls=%fused_computation | convolution fusion | flops 2172649472 | bytes 36601856 | tf_op jit(solution)/shard_map/nd,nf->df/dot_general | solution.py:46
  280.3 3.8 all-reduce.5.cloned.1.call-done
  293.8 3.3 all-to-all-start.1
  297.2 14.2 %fusion.10 = f32[9472,896]{1,0:T(8,128)} fusion(bf16[128,9472]{1,0:T(8,128)(2,1)S(1)} %copy-done, bf16[128,896]{1,0:T(8,128)(2,1)S(1)} %bitcast.72), kind=kOutput, calls=%fused_computation.21 | convolution fusion | flops 2172649472 | bytes 36601856 | tf_op jit(solution)/shard_map/nf,nd->fd/dot_general | solution.py:39
  311.4 35.5 %copy.36 = f32[896,9472]{1,0:T(8,128)} copy(f32[896,9472]{0,1:T(8,128)} %convolution_bitcast_fusion.1) | data formatting | bytes 67895296
  346.9 35.5 %copy.37 = f32[896,9472]{1,0:T(8,128)} copy(f32[896,9472]{0,1:T(8,128)} %convolution_bitcast_fusion) | data formatting | bytes 67895296
  (44 shorter events, 15.8 us)
Async XLA Ops:
  7.2 69.9 %reduce-scatter.6.cloned.1.call-start = ((), (), s32[]{:S(2)}) async-start(), calls=%async_computation.7 | async-start | bytes 6062080 | tf_op jit(solution)/shard_map/reduce_scatter | solution.py:29
  33.3 89.3 %reduce-scatter.8.cloned.1.call-start = ((), (), s32[]{:S(2)}) async-start(), calls=%async_computation.8 | async-start | bytes 6062080 | tf_op jit(solution)/shard_map/reduce_scatter | solution.py:30
  44.1 0.9 copy-start.5
  44.1 123.9 %reduce-scatter.10.cloned.1.call-start = ((), (), s32[]{:S(2)}) async-start(), calls=%async_computation.10 | async-start | bytes 6062080 | tf_op jit(solution)/shard_map/reduce_scatter | solution.py:38
  53.4 0.6 copy-start.3
  72.2 100.9 %copy-start.6 = (u32[8]{0:T(128)S(1)}, u32[8]{0:T(128)}, u32[]{:S(2)}) copy-start(u32[8]{0:T(128)} %constant.4) | copy-start | bytes 100
  72.3 121.0 %all-gather.8.cloned.1.call-start = ((), (), s32[]{:S(2)}) async-start(), calls=%async_computation.11 | async-start | bytes 3031040 | tf_op jit(solution)/shard_map/all_gather | solution.py:43
  171.8 44.7 %all-gather.6.cloned.1.call-start = ((), (), s32[]{:S(2)}) async-start(), calls=%async_computation.9 | async-start | bytes 3031040 | tf_op jit(solution)/shard_map/all_gather | solution.py:34
  172.4 67.4 %all-gather.10.cloned.1.call-start = ((), (), s32[]{:S(2)}) async-start(), calls=%async_computation.12 | async-start | bytes 3031040 | tf_op jit(solution)/shard_map/all_gather | solution.py:44
  172.9 111.2 %all-reduce.5.cloned.1.call-start = ((), (), s32[]{:S(2)}) async-start(), calls=%async_computation.13 | async-start | bytes 1835008
  239.8 12.8 %copy-start.1 = (bf16[128,9472]{1,0:T(8,128)(2,1)S(1)}, bf16[128,9472]{1,0:T(8,128)(2,1)}, u32[]{:S(2)}) copy-start(bf16[128,9472]{1,0:T(8,128)(2,1)} %all-gather.8.cloned.1.call-done) | copy-start | bytes 7274500
  252.6 14.5 %copy-start.2 = (bf16[128,9472]{1,0:T(8,128)(2,1)S(1)}, bf16[128,9472]{1,0:T(8,128)(2,1)}, u32[]{:S(2)}) copy-start(bf16[128,9472]{1,0:T(8,128)(2,1)} %all-gather.10.cloned.1.call-done) | copy-start | bytes 7274500
  267.0 17.1 %copy-start.4 = (bf16[16,4,896]{2,0,1:T(8,128)(2,1)S(1)}, bf16[16,4,896]{2,0,1:T(8,128)(2,1)}, u32[]{:S(2)}) copy-start(bf16[16,4,896]{2,0,1:T(8,128)(2,1)} %copy-done.3) | copy-start | bytes 344068
  267.0 30.1 %copy-start = (bf16[128,9472]{1,0:T(8,128)(2,1)S(1)}, bf16[128,9472]{1,0:T(8,128)(2,1)}, u32[]{:S(2)}) copy-start(bf16[128,9472]{1,0:T(8,128)(2,1)} %all-gather.6.cloned.1.call-done) | copy-start | bytes 7274500
  286.3 7.5 %all-to-all-start.3 = ((bf16[4,16,896]{2,1,0:T(8,128)(2,1)}), bf16[4,16,896]{2,1,0:T(8,128)(2,1)S(1)}, u32[]{:S(2)}, u32[]{:S(2)}) async-start(bf16[4,16,896]{2,1,0:T(8,128)(2,1)} %fusion.2), calls=%async_computation.6 | async-start | bytes 229376 | tf_op jit(solution)/shard_map/all_to_all | solution.py:24
  293.8 89.3 %all-to-all-start.1 = ((bf16[4,16,896]{2,1,0:T(8,128)(2,1)}), bf16[4,16,896]{2,1,0:T(8,128)(2,1)S(1)}, u32[]{:S(2)}, u32[]{:S(2)}) async-start(bf16[4,16,896]{2,1,0:T(8,128)(2,1)} %fusion.4), calls=%async_computation.3 | async-start | bytes 229376 | tf_op jit(solution)/shard_map/all_to_all | solution.py:24
Sparse Core Ops, SparseCore 0:
  33.4 43.6 reduce-scatter.5
  80.2 42.3 reduce-scatter.7
  125.7 42.3 reduce-scatter.9
  171.9 21.2 all-gather.7
  195.2 21.2 all-gather.5
  218.4 21.2 all-gather.9
  252.7 31.4 all-reduce.4
where the time goes:
time: 393 us; the launch traced here: 391 us
  waiting for transfers between devices  147 us (37%)
  matrix products  111 us (28%)
  local copies, waits for them, and re-layouts  75.5 us (19%)
  blocking collectives  28.2 us (7%)
  between operations  14.2 us (4%)
  other arithmetic  8.07 us (2%)
  starting transfers between devices  7.09 us (2%)
    unnamed x19, local copies, waits for them, and re-layouts  74.4 us
    reduce_scatter x1, waiting for transfers between devices, local_step(): lax.psum_scatter(jnp.einsum('nd,fd->nf', gy_cols, wd_loc, preferred_eleme...  45.5 us
    reduce_scatter x1, waiting for transfers between devices, local_step(): lax.psum_scatter(jnp.dot(x_cols, wu_loc, preferred_element_type=jnp.float...  45.5 us
    all_gather x1, waiting for transfers between devices, local_step(): gate_all = lax.all_gather(grad_gate, 'dp', axis=0, tiled=True)  19.4 us
    all_to_all x2, blocking collectives, spread_cols(): cols_mine = lax.all_to_all(rows_loc, 'dp', 1, 0, tiled=True)  17.3 us
    dot_general x1, matrix products, local_step(): jnp.einsum('nd,nf->df', x_cols, gate_all, preferred_element_type=jnp.floa...  14.5 us
    dot_general x1, matrix products, local_step(): jnp.einsum('nf,nd->fd', hidden_all, gy_cols, preferred_element_type=jnp.f...  14.2 us
    dot_general x1, matrix products, local_step(): jnp.einsum('nd,nf->df', x_cols, up_all, preferred_element_type=jnp.float32)  13.3 us
  transfers between devices with their start and end apart: 9, of which 8 were waited for; matrix products, arithmetic and copies ran while one was open for 41% of the time, Pallas kernels for 0%

commit v1 on v0

v1 whole, which is shorter than its diff:
```python
import functools

import jax
import jax.numpy as jnp
from jax import lax
from jax.experimental import pallas as pl
from jax.experimental.pallas import tpu as pltpu
from jax.sharding import PartitionSpec as P

F32 = jnp.float32
BF16 = jnp.bfloat16
CW = 256
SLOTS = 12
AHEAD = 3
KC, KD, KE = 4, 6, 8


def _dot(a, b, ca, cb):
    return lax.dot_general(a, b, (((ca,), (cb,)), ((), ())), preferred_element_type=F32)


def _exchange_kernel(nch, x_ref, gy_ref, wg_ref, wu_ref, wd_ref,
                     acc_ref, xc_out, hdd_out,
                     xc, wgb, wub, wdb, part, rdat, sx, rx, hdd,
                     wsem, tsem_s, tsem_r, ds, dr, xs, xr, gs, gr, fs, fr, osem, csem):
    dp = lax.axis_index("dp")
    tp = lax.axis_index("tp")
    xi = dp // 2
    co = dp % 2
    dd = xc.shape[2]
    mine = pl.multiple_of(co * 64, 64)
    other = pl.multiple_of((1 - co) * 64, 64)
    own = pl.multiple_of(xi * 32, 32)
    away = pl.multiple_of((1 - xi) * 32, 32)
    own_abs = pl.multiple_of(co * 64 + xi * 32, 32)
    partner = {"dp": xi * 2 + (1 - co)}
    xpeer = {"dp": (1 - xi) * 2 + co}

    def wcopies(j):
        s = j % SLOTS
        cols = pl.ds(pl.multiple_of(j * CW, CW), CW)
        return (pltpu.make_async_copy(wg_ref.at[:, cols], wgb.at[s], wsem.at[0, s]),
                pltpu.make_async_copy(wu_ref.at[:, cols], wub.at[s], wsem.at[1, s]),
                pltpu.make_async_copy(wd_ref.at[cols, :], wdb.at[s], wsem.at[2, s]))

    for j in range(AHEAD):
        for c in wcopies(j):
            c.start()

    rel = [(ax, ac, at) for ax in (0, 1) for ac in (0, 1) for at in (0, 1)][1:]

    def peer(r):
        ax, ac, at = r
        px = 1 - xi if ax else xi
        pc = 1 - co if ac else co
        pt = 1 - tp if at else tp
        return px * 2 + pc, pt

    barrier = pltpu.get_barrier_semaphore()
    for r in rel:
        q, pt = peer(r)
        pl.semaphore_signal(barrier, inc=1, device_id={"dp": q, "tp": pt},
                            device_id_type=pl.DeviceIdType.MESH)
    pl.semaphore_wait(barrier, len(rel))

    pos = pl.multiple_of(co * 64 + xi * 32 + tp * 16, 16)
    tok = []
    for n, r in enumerate(rel):
        q, pt = peer(r)
        qcols = pl.ds(pl.multiple_of(q * dd, 128), dd)
        for k, src in enumerate((x_ref, gy_ref)):
            c = pltpu.make_async_remote_copy(
                src_ref=src.at[:, qcols], dst_ref=xc.at[k, pl.ds(pos, 16), :],
                send_sem=tsem_s.at[k, n], recv_sem=tsem_r.at[k, n],
                device_id={"dp": q, "tp": pt}, device_id_type=pl.DeviceIdType.MESH)
            c.start()
            tok.append(c)
    mcols = pl.ds(pl.multiple_of(dp * dd, 128), dd)
    xc[0, pl.ds(pos, 16), :] = x_ref[:, mcols]
    xc[1, pl.ds(pos, 16), :] = gy_ref[:, mcols]
    acc_ref[...] = jnp.zeros_like(acc_ref)
    for c in tok:
        c.wait()

    def d_copy(j):
        return pltpu.make_async_remote_copy(
            src_ref=part.at[j, :, pl.ds(other, 64), :], dst_ref=rdat.at[j],
            send_sem=ds.at[j], recv_sem=dr.at[j],
            device_id=partner, device_id_type=pl.DeviceIdType.MESH)

    def x_copy(j):
        return pltpu.make_async_remote_copy(
            src_ref=sx.at[j], dst_ref=rx.at[j],
            send_sem=xs.at[j], recv_sem=xr.at[j],
            device_id=xpeer, device_id_type=pl.DeviceIdType.MESH)

    def g_copy(j):
        blk = hdd.at[j, :, pl.ds(own_abs, 32), :]
        return pltpu.make_async_remote_copy(
            src_ref=blk, dst_ref=blk, send_sem=gs.at[j], recv_sem=gr.at[j],
            device_id=xpeer, device_id_type=pl.DeviceIdType.MESH)

    def f_copy(j):
        blk = hdd.at[j, :, pl.ds(mine, 64), :]
        return pltpu.make_async_remote_copy(
            src_ref=blk, dst_ref=blk, send_sem=fs.at[j], recv_sem=fr.at[j],
            device_id=partner, device_id_type=pl.DeviceIdType.MESH)

    def o_copy(j):
        return pltpu.make_async_copy(hdd.at[j], hdd_out.at[j], osem.at[j])

    def step(i, carry):
        @pl.when(i + AHEAD < nch)
        def _():
            for c in wcopies(i + AHEAD):
                c.start()

        @pl.when(i < nch)
        def _():
            for c in wcopies(i):
                c.wait()
            s = i % SLOTS
            part[i, 0] = _dot(xc[0], wgb[s], 1, 0)
            part[i, 1] = _dot(xc[0], wub[s], 1, 0)
            part[i, 2] = _dot(xc[1], wdb[s], 1, 1)

        @pl.when((i >= KC + 1) & (i < nch + KC + 1))
        def _():
            g_copy(i - KC - 1).start()

        @pl.when((i >= 1) & (i < nch + 1))
        def _():
            j = i - 1
            d_copy(j).wait_recv()
            for k in range(3):
                sx[j, k] = (part[j, k, pl.ds(pl.multiple_of(mine + away, 32), 32), :]
                            + rdat[j, k, pl.ds(away, 32), :])

        @pl.when(i < nch)
        def _():
            d_copy(i).start()

        @pl.when((i >= KE) & (i < nch + KE))
        def _():
            j = i - KE
            s = j % SLOTS
            f_copy(j).wait_recv()
            o_copy(j).start()
            acc_ref[0] += _dot(hdd[j, 0], wdb[s], 1, 0)
            acc_ref[1] += _dot(hdd[j, 1], wgb[s], 1, 1) + _dot(hdd[j, 2], wub[s], 1, 1)

        @pl.when((i >= 1) & (i < nch + 1))
        def _():
            x_copy(i - 1).start()

        @pl.when((i >= KD) & (i < nch + KD))
        def _():
            g_copy(i - KD).wait_recv()
            f_copy(i - KD).start()

        @pl.when((i >= KC) & (i < nch + KC))
        def _():
            j = i - KC
            x_copy(j).wait_recv()
            a, b, g = (part[j, k, pl.ds(own_abs, 32), :] + rdat[j, k, pl.ds(own, 32), :] + rx[j, k]
                       for k in range(3))
            sig = jax.nn.sigmoid(a)
            silu = a * sig
            hdd[j, 0, pl.ds(own_abs, 32), :] = (silu * b).astype(BF16)
            deriv = sig * (1.0 + a * (1.0 - sig))
            hdd[j, 1, pl.ds(own_abs, 32), :] = (g * b * deriv).astype(BF16)
            hdd[j, 2, pl.ds(own_abs, 32), :] = (g * silu).astype(BF16)

        return carry

    lax.fori_loop(0, nch + KE, step, 0)

    cc = pltpu.make_async_copy(xc, xc_out, csem)
    cc.start()

    def finish(j, carry):
        d_copy(j).wait_send()
        x_copy(j).wait_send()
        g_copy(j).wait_send()
        f_copy(j).wait_send()
        o_copy(j).wait()
        return carry

    lax.fori_loop(0, nch, finish, 0)
    cc.wait()


def _exchange(x_loc, gy_loc, wg, wu, wd):
    dd, ff = wg.shape
    nch = ff // CW
    tok = 128
    vm = pl.BlockSpec(memory_space=pltpu.VMEM)
    hbm = pl.BlockSpec(memory_space=pl.ANY)
    dma = pltpu.SemaphoreType.DMA
    return pl.pallas_call(
        functools.partial(_exchange_kernel, nch),
        out_shape=(jax.ShapeDtypeStruct((2, tok, dd), F32),
                   jax.ShapeDtypeStruct((2, tok, dd), BF16),
                   jax.ShapeDtypeStruct((nch, 3, tok, CW), BF16)),
        in_specs=[vm, vm, hbm, hbm, hbm],
        out_specs=(vm, hbm, hbm),
        scratch_shapes=[
            pltpu.VMEM((2, tok, dd), BF16),
            pltpu.VMEM((SLOTS, dd, CW), BF16),
            pltpu.VMEM((SLOTS, dd, CW), BF16),
            pltpu.VMEM((SLOTS, CW, dd), BF16),
            pltpu.VMEM((nch, 3, tok, CW), F32),
            pltpu.VMEM((nch, 3, 64, CW), F32),
            pltpu.VMEM((nch, 3, 32, CW), F32),
            pltpu.VMEM((nch, 3, 32, CW), F32),
            pltpu.VMEM((nch, 3, tok, CW), BF16),
            dma((3, SLOTS)), dma((2, 7)), dma((2, 7)),
            dma((nch,)), dma((nch,)), dma((nch,)), dma((nch,)),
            dma((nch,)), dma((nch,)), dma((nch,)), dma((nch,)),
            dma((nch,)), dma(()),
        ],
        compiler_params=pltpu.CompilerParams(
            collective_id=0, has_side_effects=True, vmem_limit_bytes=66 * 1000 * 1000),
        cost_estimate=pl.CostEstimate(flops=12 * tok * dd * ff, bytes_accessed=6 * dd * ff,
                                      transcendentals=0),
        name="exchange",
    )(x_loc, gy_loc, wg, wu, wd)


def _down_kernel(gy_ref, h_ref, o_ref):
    o_ref[...] = _dot(h_ref[0, 0], gy_ref[0], 0, 0)


def _up_kernel(xt_ref, d_ref, og_ref, ou_ref):
    xt = xt_ref[...]
    og_ref[...] = _dot(xt, d_ref[0, 1], 1, 0)
    ou_ref[...] = _dot(xt, d_ref[0, 2], 1, 0)


def _grads(xc, hdd):
    nch = hdd.shape[0]
    _, tok, dd = xc.shape
    ff = nch * CW
    gwd = pl.pallas_call(
        _down_kernel,
        grid=(nch,),
        out_shape=jax.ShapeDtypeStruct((ff, dd), F32),
        in_specs=[pl.BlockSpec((1, tok, dd), lambda i: (1, 0, 0)),
                  pl.BlockSpec((1, 1, tok, CW), lambda i: (i, 0, 0, 0))],
        out_specs=pl.BlockSpec((CW, dd), lambda i: (i, 0)),
        cost_estimate=pl.CostEstimate(flops=2 * tok * dd * ff, bytes_accessed=4 * dd * ff,
                                      transcendentals=0),
        name="grad_down",
    )(xc, hdd)
    gwg, gwu = pl.pallas_call(
        _up_kernel,
        grid=(nch,),
        out_shape=(jax.ShapeDtypeStruct((dd, ff), F32), jax.ShapeDtypeStruct((dd, ff), F32)),
        in_specs=[pl.BlockSpec((dd, tok), lambda i: (0, 0)),
                  pl.BlockSpec((1, 3, tok, CW), lambda i: (i, 0, 0, 0))],
        out_specs=(pl.BlockSpec((dd, CW), lambda i: (0, i)), pl.BlockSpec((dd, CW), lambda i: (0, i))),
        cost_estimate=pl.CostEstimate(flops=4 * tok * dd * ff, bytes_accessed=8 * dd * ff,
                                      transcendentals=0),
        name="grad_up",
    )(xc[0].T, hdd)
    return gwg, gwu, gwd


def solution(mesh):
    def local_step(x_loc, wg, wu, wd, gy_loc):
        acc, xc, hdd = _exchange(x_loc, gy_loc, wg, wu, wd)
        dd = wg.shape[0]
        tp = lax.axis_index("tp")
        acc5 = acc.reshape(2, 2, 2, 2, 16, dd)
        keep = lax.dynamic_index_in_dim(acc5, tp, 3, keepdims=False)
        give = lax.dynamic_index_in_dim(acc5, 1 - tp, 3, keepdims=False)
        got = lax.ppermute(give, "tp", [(0, 1), (1, 0)])
        resid = lax.dynamic_index_in_dim(xc.reshape(2, 2, 2, 2, 16, dd), tp, 3, keepdims=False)
        rows = (keep + got + resid.astype(F32)).astype(BF16)
        rows = rows.transpose(2, 1, 0, 3, 4).reshape(4, 2, 16, dd)
        rows = lax.all_to_all(rows, "dp", 0, 0, tiled=True)
        rows = rows.transpose(1, 2, 0, 3).reshape(2, 16, 4 * dd)
        gwg, gwu, gwd = _grads(xc, hdd)
        return rows[0], rows[1], gwg, gwu, gwd

    row_spec = P(("dp", "tp"), None)
    up_spec = P("dp", "tp")
    down_spec = P("tp", "dp")
    return jax.shard_map(local_step, mesh=mesh,
                         in_specs=(row_spec, up_spec, up_spec, down_spec, row_spec),
                         out_specs=(row_spec, row_spec, up_spec, up_spec, down_spec),
                         check_vma=False)
```

time: 393 us -> 216 us (0.55)
  Pallas kernels: 0 us -> 202 us
  waiting for transfers between devices: 147 us -> 0.01 us
  matrix products: 111 us -> 0 us
  local copies, waits for them, and re-layouts: 75.5 us -> 4.73 us
  blocking collectives: 28.2 us -> 0 us
  between operations: 14.2 us -> 0.7 us
  other arithmetic: 8.07 us -> 0.75 us
    pallas_call x0 -> x3, Pallas kernels: none -> 202 us  [the longest x1 139 us: _exchange(): pl.pallas_call(functools.partial(_exchange_kernel, nch), out_shape=(jax.S...]
    dot_general x9 -> x0, matrix products: 111 us -> none  [the longest x1 14.5 us: local_step(): jnp.einsum('nd,nf->df', x_cols, gate_all, preferred_element_type=jnp.floa...]
    reduce_scatter x3 -> x0, waiting for transfers between devices: 95.7 us -> none  [the longest x1 45.5 us: local_step(): lax.psum_scatter(jnp.einsum('nd,fd->nf', gy_cols, wd_loc, preferred_eleme...]
    unnamed x19 -> x4, local copies, waits for them, and re-layouts: 74.4 us -> 1.33 us
    all_gather x3 -> x0, waiting for transfers between devices: 44.1 us -> none  [the longest x1 19.4 us: local_step(): gate_all = lax.all_gather(grad_gate, 'dp', axis=0, tiled=True)]
    all_to_all x2 -> x0, blocking collectives: 17.3 us -> none  [spread_cols(): cols_mine = lax.all_to_all(rows_loc, 'dp', 1, 0, tiled=True)]
    all_gather x2 -> x0, blocking collectives: 10.9 us -> none  [spread_cols(): gathered = lax.all_gather(cols_mine, 'tp', axis=1)]
    convert_element_type x3 -> x1, other arithmetic: 8.07 us -> 0.75 us  [local_step(): rows = (keep + got + resid.astype(F32)).astype(BF16)]
  transfers between devices with their start and end apart: 9 -> 2, of which waited for: 8 -> 0; matrix products, arithmetic and copies ran while one was open for 41% -> 1% of each run, Pallas kernels for 0% -> 30%
where the time goes in v1:
time: 216 us; the launch traced here: 213 us
  Pallas kernels  202 us (94%)
  starting transfers between devices  4.89 us (2%)
  local copies, waits for them, and re-layouts  4.73 us (2%)
    pallas_call x1, Pallas kernels, _exchange(): pl.pallas_call(functools.partial(_exchange_kernel, nch), out_shape=(jax.S...  139 us
    pallas_call x1, Pallas kernels, _grads(): pl.pallas_call(_up_kernel, grid=(nch,), out_shape=(jax.ShapeDtypeStruct((...  35.3 us
    pallas_call x1, Pallas kernels, _grads(): pl.pallas_call(_down_kernel, grid=(nch,), out_shape=jax.ShapeDtypeStruct(...  27.7 us
  transfers between devices with their start and end apart: 2, of which 0 were waited for; matrix products, arithmetic and copies ran while one was open for 1% of the time, Pallas kernels for 30%

profile of v1, /device:TPU:0, one launch (start us, length us, event | category | flops | bytes accessed | tf_op | source)
XLA Modules:
  0.0 213.3 jit_solution(255888788651601787)
XLA Ops:
  0.6 139.3 %exchange.1 = (f32[2,128,896]{2,1,0:T(8,128)}, bf16[2,128,896]{2,1,0:T(8,128)(2,1)}, bf16[37,3,128,256]{3,2,1,0:T(8,128)(2,1)}) custom-call(bf16[16,3584]{1,0:T(8,128)(2,1)} %x_ref.1, bf16[16,3584]{1,0:T(8,128)(2,1)} %gy_ref.1, bf16[896,9472]{1,0:T(8,128)(2,1)} %wg_ref.1, bf16[896,9472]{1,0:T(8,128)(2,1)} %wu_ref.1, bf16[9472,896]{1,0:T(8,128)(2,1)} %wd_ref.1), custom_call_target="tpu_custom_call" | custom-call | flops 13035896832 | bytes 50921472 | tf_op jit(solution)/shard_map/exchange/pallas_call | solution.py:200
  139.9 0.0 copy-start
  139.9 1.3 constant_dynamic-slice_fusion.2
  141.3 1.5 collective-permute-start
  142.8 1.3 copy.20
  144.0 0.7 slice_bitcast_fusion.xt_ref
  144.8 35.3 %grad_up.1 = (f32[896,9472]{1,0:T(8,128)}, f32[896,9472]{1,0:T(8,128)}) custom-call(bf16[896,128]{1,0:T(8,128)(2,1)} %slice_bitcast_fusion.xt_ref, bf16[37,3,128,256]{3,2,1,0:T(8,128)(2,1)} %get-tuple-element.12.d_ref.h_ref), custom_call_target="tpu_custom_call" | custom-call | flops 4345298944 | bytes 67895296 | tf_op jit(solution)/shard_map/grad_up/pallas_call | solution.py:255
  180.0 0.0 collective-permute-done
  180.0 0.0 copy-done
  180.0 0.8 fusion
  180.8 3.4 %all-to-all-start = ((bf16[4,2,16,896]{3,2,1,0:T(8,128)(2,1)}), bf16[4,2,16,896]{3,2,1,0:T(8,128)(2,1)S(1)}, u32[]{:S(2)}, u32[]{:S(2)}) async-start(bf16[4,2,16,896]{3,2,1,0:T(8,128)(2,1)} %bitcast.6), calls=%async_computation | async-start | bytes 458752 | tf_op jit(solution)/shard_map/all_to_all | solution.py:281
  184.2 27.7 %grad_down.1 = f32[9472,896]{1,0:T(8,128)} custom-call(bf16[2,128,896]{2,1,0:T(8,128)(2,1)} %get-tuple-element.11.gy_ref, bf16[37,3,128,256]{3,2,1,0:T(8,128)(2,1)} %get-tuple-element.12.d_ref.h_ref), custom_call_target="tpu_custom_call" | custom-call | flops 2172649472 | bytes 33947648 | tf_op jit(solution)/shard_map/grad_down/pallas_call | solution.py:244
  211.9 0.0 all-to-all-done
  211.9 0.7 copy.23
  212.7 0.7 copy.22
  (4 shorter events, 0.1 us)
Async XLA Ops:
  139.9 40.1 %copy-start = (bf16[2,128,896]{2,1,0:T(8,128)(2,1)S(1)}, bf16[2,128,896]{2,1,0:T(8,128)(2,1)}, u32[]{:S(2)}) copy-start(bf16[2,128,896]{2,1,0:T(8,128)(2,1)} %get-tuple-element.11.gy_ref) | copy-start | bytes 1376260
  141.3 38.8 %collective-permute-start = (f32[2,2,2,16,896]{4,3,0,1,2:T(8,128)S(1)}, f32[2,2,2,16,896]{4,3,0,1,2:T(8,128)S(1)}, u32[]{:S(2)}, u32[]{:S(2)}) collective-permute-start(f32[2,2,2,16,896]{4,3,0,1,2:T(8,128)S(1)} %bitcast.31), channel_id=1, source_target_pairs={{0,4},{4,0},{1,5},{5,1},{2,6},{6,2},{3,7},{7,3}} | collective-permute-start | bytes 1376264 | tf_op jit(solution)/shard_map/ppermute | solution.py:277
  180.8 31.1 %all-to-all-start = ((bf16[4,2,16,896]{3,2,1,0:T(8,128)(2,1)}), bf16[4,2,16,896]{3,2,1,0:T(8,128)(2,1)S(1)}, u32[]{:S(2)}, u32[]{:S(2)}) async-start(bf16[4,2,16,896]{3,2,1,0:T(8,128)(2,1)} %bitcast.6), calls=%async_computation | async-start | bytes 458752 | tf_op jit(solution)/shard_map/all_to_all | solution.py:281

commit v2 on v1

--- a/solution.py
+++ b/solution.py
@@ -11,8 +11,9 @@
 BF16 = jnp.bfloat16
 CW = 256
 SLOTS = 12
+RING = 8
 AHEAD = 3
-KC, KD, KE = 4, 6, 8
+KC, KD, KE = 4, 6, 7
 
 
 def _dot(a, b, ca, cb):
@@ -20,8 +21,8 @@
 
 
 def _exchange_kernel(nch, x_ref, gy_ref, wg_ref, wu_ref, wd_ref,
-                     acc_ref, xc_out, hdd_out,
-                     xc, wgb, wub, wdb, part, rdat, sx, rx, hdd,
+                     give, xc_out, hdd_out,
+                     acc_ref, xc, wgb, wub, wdb, part, rdat, sx, rx, hdd,
                      wsem, tsem_s, tsem_r, ds, dr, xs, xr, gs, gr, fs, fr, osem, csem):
     dp = lax.axis_index("dp")
     tp = lax.axis_index("tp")
@@ -65,10 +66,10 @@
 
     pos = pl.multiple_of(co * 64 + xi * 32 + tp * 16, 16)
     tok = []
-    for n, r in enumerate(rel):
-        q, pt = peer(r)
-        qcols = pl.ds(pl.multiple_of(q * dd, 128), dd)
-        for k, src in enumerate((x_ref, gy_ref)):
+    for k, src in enumerate((x_ref, gy_ref)):
+        for n, r in enumerate(rel):
+            q, pt = peer(r)
+            qcols = pl.ds(pl.multiple_of(q * dd, 128), dd)
             c = pltpu.make_async_remote_copy(
                 src_ref=src.at[:, qcols], dst_ref=xc.at[k, pl.ds(pos, 16), :],
                 send_sem=tsem_s.at[k, n], recv_sem=tsem_r.at[k, n],
@@ -79,7 +80,7 @@
     xc[0, pl.ds(pos, 16), :] = x_ref[:, mcols]
     xc[1, pl.ds(pos, 16), :] = gy_ref[:, mcols]
     acc_ref[...] = jnp.zeros_like(acc_ref)
-    for c in tok:
+    for c in tok[:len(rel)]:
         c.wait()
 
     def d_copy(j):
@@ -122,6 +123,12 @@
             s = i % SLOTS
             part[i, 0] = _dot(xc[0], wgb[s], 1, 0)
             part[i, 1] = _dot(xc[0], wub[s], 1, 0)
+
+            @pl.when(i == 0)
+            def _():
+                for c in tok[len(rel):]:
+                    c.wait()
+
             part[i, 2] = _dot(xc[1], wdb[s], 1, 1)
 
         @pl.when((i >= KC + 1) & (i < nch + KC + 1))
@@ -177,6 +184,10 @@
 
     cc = pltpu.make_async_copy(xc, xc_out, csem)
     cc.start()
+    for t in range(2):
+        for q in range(4):
+            row = (q % 2) * 64 + (q // 2) * 32 + t * 16
+            give[t * 4 + q] = acc_ref[:, row:row + 16, :]
 
     def finish(j, carry):
         d_copy(j).wait_send()
@@ -199,12 +210,13 @@
     dma = pltpu.SemaphoreType.DMA
     return pl.pallas_call(
         functools.partial(_exchange_kernel, nch),
-        out_shape=(jax.ShapeDtypeStruct((2, tok, dd), F32),
+        out_shape=(jax.ShapeDtypeStruct((8, 2, 16, dd), F32),
                    jax.ShapeDtypeStruct((2, tok, dd), BF16),
                    jax.ShapeDtypeStruct((nch, 3, tok, CW), BF16)),
         in_specs=[vm, vm, hbm, hbm, hbm],
         out_specs=(vm, hbm, hbm),
         scratch_shapes=[
+            pltpu.VMEM((2, tok, dd), F32),
             pltpu.VMEM((2, tok, dd), BF16),
             pltpu.VMEM((SLOTS, dd, CW), BF16),
             pltpu.VMEM((SLOTS, dd, CW), BF16),
@@ -227,61 +239,87 @@
     )(x_loc, gy_loc, wg, wu, wd)
 
 
-def _down_kernel(gy_ref, h_ref, o_ref):
-    o_ref[...] = _dot(h_ref[0, 0], gy_ref[0], 0, 0)
-
-
-def _up_kernel(xt_ref, d_ref, og_ref, ou_ref):
-    xt = xt_ref[...]
-    og_ref[...] = _dot(xt, d_ref[0, 1], 1, 0)
-    ou_ref[...] = _dot(xt, d_ref[0, 2], 1, 0)
+def _grads_kernel(nch, xc_ref, hdd_ref, gwg_ref, gwu_ref, gwd_ref,
+                  hdd, xt, og, ou, od, isem, osem):
+    def fetch(j):
+        return pltpu.make_async_copy(hdd_ref.at[j], hdd.at[j], isem.at[j])
+
+    def put(j):
+        s = j % RING
+        cols = pl.ds(pl.multiple_of(j * CW, CW), CW)
+        return (pltpu.make_async_copy(og.at[s], gwg_ref.at[:, cols], osem.at[0, s]),
+                pltpu.make_async_copy(ou.at[s], gwu_ref.at[:, cols], osem.at[1, s]),
+                pltpu.make_async_copy(od.at[s], gwd_ref.at[cols, :], osem.at[2, s]))
+
+    def start_fetch(j, carry):
+        fetch(j).start()
+        return carry
+
+    lax.fori_loop(0, nch, start_fetch, 0)
+    xt[...] = xc_ref[0].T
+
+    def step(j, carry):
+        s = j % RING
+
+        @pl.when(j >= RING)
+        def _():
+            for c in put(j - RING):
+                c.wait()
+
+        fetch(j).wait()
+        og[s] = _dot(xt[...], hdd[j, 1], 1, 0)
+        ou[s] = _dot(xt[...], hdd[j, 2], 1, 0)
+        od[s] = _dot(hdd[j, 0], xc_ref[1], 0, 0)
+        for c in put(j):
+            c.start()
+        return carry
+
+    lax.fori_loop(0, nch, step, 0)
+
+    def drain(j, carry):
+        for c in put(j):
+            c.wait()
+        return carry
+
+    lax.fori_loop(nch - RING, nch, drain, 0)
 
 
 def _grads(xc, hdd):
     nch = hdd.shape[0]
     _, tok, dd = xc.shape
     ff = nch * CW
-    gwd = pl.pallas_call(
-        _down_kernel,
-        grid=(nch,),
-        out_shape=jax.ShapeDtypeStruct((ff, dd), F32),
-        in_specs=[pl.BlockSpec((1, tok, dd), lambda i: (1, 0, 0)),
-                  pl.BlockSpec((1, 1, tok, CW), lambda i: (i, 0, 0, 0))],
-        out_specs=pl.BlockSpec((CW, dd), lambda i: (i, 0)),
-        cost_estimate=pl.CostEstimate(flops=2 * tok * dd * ff, bytes_accessed=4 * dd * ff,
+    hbm = pl.BlockSpec(memory_space=pl.ANY)
+    dma = pltpu.SemaphoreType.DMA
+    return pl.pallas_call(
+        functools.partial(_grads_kernel, nch),
+        out_shape=(jax.ShapeDtypeStruct((dd, ff), F32), jax.ShapeDtypeStruct((dd, ff), F32),
+                   jax.ShapeDtypeStruct((ff, dd), F32)),
+        in_specs=[pl.BlockSpec(memory_space=pltpu.VMEM), hbm],
+        out_specs=(hbm, hbm, hbm),
+        scratch_shapes=[
+            pltpu.VMEM(hdd.shape, BF16), pltpu.VMEM((dd, tok), BF16),
+            pltpu.VMEM((RING, dd, CW), F32), pltpu.VMEM((RING, dd, CW), F32),
+            pltpu.VMEM((RING, CW, dd), F32),
+            dma((nch,)), dma((3, RING)),
+        ],
+        compiler_params=pltpu.CompilerParams(vmem_limit_bytes=66 * 1000 * 1000),
+        cost_estimate=pl.CostEstimate(flops=6 * tok * dd * ff, bytes_accessed=12 * dd * ff,
                                       transcendentals=0),
-        name="grad_down",
+        name="grads",
     )(xc, hdd)
-    gwg, gwu = pl.pallas_call(
-        _up_kernel,
-        grid=(nch,),
-        out_shape=(jax.ShapeDtypeStruct((dd, ff), F32), jax.ShapeDtypeStruct((dd, ff), F32)),
-        in_specs=[pl.BlockSpec((dd, tok), lambda i: (0, 0)),
-                  pl.BlockSpec((1, 3, tok, CW), lambda i: (i, 0, 0, 0))],
-        out_specs=(pl.BlockSpec((dd, CW), lambda i: (0, i)), pl.BlockSpec((dd, CW), lambda i: (0, i))),
-        cost_estimate=pl.CostEstimate(flops=4 * tok * dd * ff, bytes_accessed=8 * dd * ff,
-                                      transcendentals=0),
-        name="grad_up",
-    )(xc[0].T, hdd)
-    return gwg, gwu, gwd
 
 
 def solution(mesh):
     def local_step(x_loc, wg, wu, wd, gy_loc):
-        acc, xc, hdd = _exchange(x_loc, gy_loc, wg, wu, wd)
-        dd = wg.shape[0]
-        tp = lax.axis_index("tp")
-        acc5 = acc.reshape(2, 2, 2, 2, 16, dd)
-        keep = lax.dynamic_index_in_dim(acc5, tp, 3, keepdims=False)
-        give = lax.dynamic_index_in_dim(acc5, 1 - tp, 3, keepdims=False)
-        got = lax.ppermute(give, "tp", [(0, 1), (1, 0)])
-        resid = lax.dynamic_index_in_dim(xc.reshape(2, 2, 2, 2, 16, dd), tp, 3, keepdims=False)
-        rows = (keep + got + resid.astype(F32)).astype(BF16)
-        rows = rows.transpose(2, 1, 0, 3, 4).reshape(4, 2, 16, dd)
-        rows = lax.all_to_all(rows, "dp", 0, 0, tiled=True)
-        rows = rows.transpose(1, 2, 0, 3).reshape(2, 16, 4 * dd)
+        give, xc, hdd = _exchange(x_loc, gy_loc, wg, wu, wd)
+        got = lax.all_to_all(give, ("tp", "dp"), 0, 0, tiled=True)
         gwg, gwu, gwd = _grads(xc, hdd)
-        return rows[0], rows[1], gwg, gwu, gwd
+
+        def own_rows(k, resid):
+            both = [got[q, k] + got[q + 4, k] for q in range(4)]
+            return (jnp.concatenate(both, axis=1) + resid.astype(F32)).astype(BF16)
+
+        return own_rows(0, x_loc), own_rows(1, gy_loc), gwg, gwu, gwd
 
     row_spec = P(("dp", "tp"), None)
     up_spec = P("dp", "tp")

time: 216 us -> 181 us (0.84); the launches traced: 213 us -> 181 us
  Pallas kernels: 202 us -> 176 us
  local copies, waits for them, and re-layouts: 4.73 us -> 0.01 us
  starting transfers between devices: 4.89 us -> 2.43 us
    pallas_call x2 -> x1, Pallas kernels: 63 us -> 34.8 us  [_grads(): pl.pallas_call(functools.partial(_grads_kernel, nch), out_shape=(jax.Shap...]
  transfers between devices with their start and end apart: 2 -> 1, of which waited for: 0 -> 0; matrix products, arithmetic and copies ran while one was open for 1% -> 0% of each run, Pallas kernels for 30% -> 19%
where the time goes in v2:
time: 181 us
  Pallas kernels  176 us (97%)
  starting transfers between devices  2.43 us (1%)
    pallas_call x1, Pallas kernels, _exchange(): pl.pallas_call(functools.partial(_exchange_kernel, nch), out_shape=(jax.S...  141 us
    pallas_call x1, Pallas kernels, _grads(): pl.pallas_call(functools.partial(_grads_kernel, nch), out_shape=(jax.Shap...  34.8 us
  transfers between devices with their start and end apart: 1, of which 0 were waited for; matrix products, arithmetic and copies ran while one was open for 0% of the time, Pallas kernels for 19%

profile of v2, /device:TPU:0, one launch (start us, length us, event | category | flops | bytes accessed | tf_op | source)
XLA Modules:
  0.0 180.6 jit_solution(13395831642933812554)
XLA Ops:
  0.6 141.0 %exchange.1 = (f32[8,2,16,896]{3,2,1,0:T(8,128)}, bf16[2,128,896]{2,1,0:T(8,128)(2,1)}, bf16[37,3,128,256]{3,2,1,0:T(8,128)(2,1)}) custom-call(bf16[16,3584]{1,0:T(8,128)(2,1)} %x_ref.1, bf16[16,3584]{1,0:T(8,128)(2,1)} %gy_ref.1, bf16[896,9472]{1,0:T(8,128)(2,1)} %wg_ref.1, bf16[896,9472]{1,0:T(8,128)(2,1)} %wu_ref.1, bf16[9472,896]{1,0:T(8,128)(2,1)} %wd_ref.1), custom_call_target="tpu_custom_call" | custom-call | flops 13035896832 | bytes 50921472 | tf_op jit(solution)/shard_map/exchange/pallas_call | solution.py:211
  141.7 0.0 copy-start
  141.7 2.4 %all-to-all-start = ((f32[8,2,16,896]{3,2,1,0:T(8,128)}), f32[8,2,16,896]{3,2,1,0:T(8,128)S(1)}, u32[]{:S(2)}, u32[]{:S(2)}) async-start(f32[8,2,16,896]{3,2,1,0:T(8,128)} %get-tuple-element.11), calls=%async_computation | async-start | bytes 1835008 | tf_op jit(solution)/shard_map/all_to_all | solution.py:315
  144.1 34.8 %grads.1 = (f32[896,9472]{1,0:T(8,128)}, f32[896,9472]{1,0:T(8,128)}, f32[9472,896]{1,0:T(8,128)}) custom-call(bf16[2,128,896]{2,1,0:T(8,128)(2,1)} %get-tuple-element.12.xc_ref, bf16[37,3,128,256]{3,2,1,0:T(8,128)(2,1)} %get-tuple-element.13.hdd_ref), custom_call_target="tpu_custom_call" | custom-call | flops 6517948416 | bytes 101842944 | tf_op jit(solution)/shard_map/grads/pallas_call | solution.py:293
  178.9 0.0 all-to-all-done
  178.9 0.1 fusion.5
  179.0 0.0 copy-done
  179.0 1.6 fusion
Async XLA Ops:
  141.7 37.3 %copy-start = (bf16[16,3584]{1,0:T(8,128)(2,1)S(1)}, bf16[16,3584]{1,0:T(8,128)(2,1)}, u32[]{:S(2)}) copy-start(bf16[16,3584]{1,0:T(8,128)(2,1)} %x_ref.1) | copy-start | bytes 344068
  141.7 37.2 %all-to-all-start = ((f32[8,2,16,896]{3,2,1,0:T(8,128)}), f32[8,2,16,896]{3,2,1,0:T(8,128)S(1)}, u32[]{:S(2)}, u32[]{:S(2)}) async-start(f32[8,2,16,896]{3,2,1,0:T(8,128)} %get-tuple-element.11), calls=%async_computation | async-start | bytes 1835008 | tf_op jit(solution)/shard_map/all_to_all | solution.py:315

commit v3 on v2

v3 whole, which is shorter than its diff:
```python
import functools

import jax
import jax.numpy as jnp
from jax import lax
from jax.experimental import pallas as pl
from jax.experimental.pallas import tpu as pltpu
from jax.sharding import PartitionSpec as P

F32 = jnp.float32
BF16 = jnp.bfloat16
CW = 256
NFULL = 26
REST_AT = 8
GRAD_VMEM = 66 * 1000 * 1000
SLOTS2 = 3
AHEAD2 = 2
SLOTS = 11
RING = 8
AHEAD = 3
KC, KD, KE = 4, 6, 7


def _dot(a, b, ca, cb):
    return lax.dot_general(a, b, (((ca,), (cb,)), ((), ())), preferred_element_type=F32)


def _sigmoid_parts(a, b, g):
    sig = jax.nn.sigmoid(a)
    silu = a * sig
    deriv = sig * (1.0 + a * (1.0 - sig))
    return (silu * b).astype(BF16), (g * b * deriv).astype(BF16), (g * silu).astype(BF16)


def _remote(src, dst, send, recv, dev):
    return pltpu.make_async_remote_copy(src_ref=src, dst_ref=dst, send_sem=send, recv_sem=recv,
                                        device_id=dev, device_id_type=pl.DeviceIdType.MESH)


def _exchange_kernel(nch, nfull, x_ref, gy_ref, wg_ref, wu_ref, wd_ref,
                     acc, xc_out, hdd_out, give_out, keep_out,
                     xc, wgb, wub, wdb, wgb2, wub2, wdb2, part, rdat, sx, rx, hdd, give, keep,
                     wsem, wsem2, tsem_s, tsem_r, ds, dr, xs, xr, gs, gr, fs, fr, osem, csem, ksem):
    nrest = nch - nfull
    dp = lax.axis_index("dp")
    tp = lax.axis_index("tp")
    xi = dp // 2
    co = dp % 2
    dd = xc.shape[2]
    mine = pl.multiple_of(co * 64, 64)
    other = pl.multiple_of((1 - co) * 64, 64)
    own = pl.multiple_of(xi * 32, 32)
    away = pl.multiple_of((1 - xi) * 32, 32)
    own_abs = pl.multiple_of(co * 64 + xi * 32, 32)
    away_abs = pl.multiple_of(co * 64 + (1 - xi) * 32, 32)
    partner = {"dp": xi * 2 + (1 - co)}
    xpeer = {"dp": (1 - xi) * 2 + co}

    def wcopies(j, s, bufs, sem):
        cols = pl.ds(pl.multiple_of(j * CW, CW), CW)
        return (pltpu.make_async_copy(wg_ref.at[:, cols], bufs[0].at[s], sem.at[0, s]),
                pltpu.make_async_copy(wu_ref.at[:, cols], bufs[1].at[s], sem.at[1, s]),
                pltpu.make_async_copy(wd_ref.at[cols, :], bufs[2].at[s], sem.at[2, s]))

    def first_w(j):
        return wcopies(j, j % SLOTS, (wgb, wub, wdb), wsem)

    def rest_w(r):
        return wcopies(nfull + r, r % SLOTS2, (wgb2, wub2, wdb2), wsem2)

    for j in range(AHEAD):
        for c in first_w(j):
            c.start()

    rel = [(ax, ac, at) for ax in (0, 1) for ac in (0, 1) for at in (0, 1)][1:]

    def peer(r):
        ax, ac, at = r
        px = 1 - xi if ax else xi
        pc = 1 - co if ac else co
        pt = 1 - tp if at else tp
        return px * 2 + pc, pt

    barrier = pltpu.get_barrier_semaphore()
    for r in rel:
        q, pt = peer(r)
        pl.semaphore_signal(barrier, inc=1, device_id={"dp": q, "tp": pt},
                            device_id_type=pl.DeviceIdType.MESH)
    pl.semaphore_wait(barrier, len(rel))

    pos = pl.multiple_of(co * 64 + xi * 32 + tp * 16, 16)
    tok = []
    for k, src in enumerate((x_ref, gy_ref)):
        for n, r in enumerate(rel):
            q, pt = peer(r)
            qcols = pl.ds(pl.multiple_of(q * dd, 128), dd)
            c = _remote(src.at[:, qcols], xc.at[k, pl.ds(pos, 16), :],
                        tsem_s.at[k, n], tsem_r.at[k, n], {"dp": q, "tp": pt})
            c.start()
            tok.append(c)
    mcols = pl.ds(pl.multiple_of(dp * dd, 128), dd)
    xc[0, pl.ds(pos, 16), :] = x_ref[:, mcols]
    xc[1, pl.ds(pos, 16), :] = gy_ref[:, mcols]
    acc[...] = jnp.zeros_like(acc)
    for c in tok[:len(rel)]:
        c.wait()

    def d_copy(j):
        return _remote(part.at[j, :, pl.ds(other, 64), :], rdat.at[j], ds.at[j], dr.at[j], partner)

    def x_copy(j):
        return _remote(sx.at[j], rx.at[j], xs.at[j], xr.at[j], xpeer)

    def g_copy(j):
        blk = hdd.at[j, :, pl.ds(own_abs, 32), :]
        return _remote(blk, blk, gs.at[j], gr.at[j], xpeer)

    def f_copy(j):
        blk = hdd.at[j, :, pl.ds(mine, 64), :]
        return _remote(blk, blk, fs.at[j], fr.at[j], partner)

    def o_copy(j):
        return pltpu.make_async_copy(hdd.at[j], hdd_out.at[j], osem.at[j])

    def k_copies(r):
        return (pltpu.make_async_copy(give.at[r], give_out.at[r], ksem.at[0, r]),
                pltpu.make_async_copy(keep.at[r], keep_out.at[r], ksem.at[1, r]))

    def step(i, carry):
        rest = i - REST_AT

        @pl.when(i + AHEAD < nfull)
        def _():
            for c in first_w(i + AHEAD):
                c.start()

        @pl.when((rest + AHEAD2 >= 0) & (rest + AHEAD2 < nrest))
        def _():
            for c in rest_w(rest + AHEAD2):
                c.start()

        @pl.when(i < nfull)
        def _():
            for c in first_w(i):
                c.wait()
            s = i % SLOTS
            part[i, 0] = _dot(xc[0], wgb[s], 1, 0)
            part[i, 1] = _dot(xc[0], wub[s], 1, 0)

            @pl.when(i == 0)
            def _():
                for c in tok[len(rel):]:
                    c.wait()

            part[i, 2] = _dot(xc[1], wdb[s], 1, 1)

        @pl.when((i >= KC + 1) & (i < nfull + KC + 1))
        def _():
            g_copy(i - KC - 1).start()

        @pl.when((i >= 1) & (i < nfull + 1))
        def _():
            j = i - 1
            d_copy(j).wait_recv()
            for k in range(3):
                sx[j, k] = part[j, k, pl.ds(away_abs, 32), :] + rdat[j, k, pl.ds(away, 32), :]

        @pl.when(i < nfull)
        def _():
            d_copy(i).start()

        @pl.when((i >= KE) & (i < nfull + KE))
        def _():
            j = i - KE
            s = j % SLOTS
            f_copy(j).wait_recv()
            o_copy(j).start()
            acc[0] += _dot(hdd[j, 0], wdb[s], 1, 0)
            acc[1] += _dot(hdd[j, 1], wgb[s], 1, 1) + _dot(hdd[j, 2], wub[s], 1, 1)

        @pl.when((i >= 1) & (i < nfull + 1))
        def _():
            x_copy(i - 1).start()

        @pl.when((rest >= 0) & (rest < nrest))
        def _():
            for c in rest_w(rest):
                c.wait()
            s = rest % SLOTS2
            j = nfull + rest
            part[j, 0] = _dot(xc[0], wgb2[s], 1, 0)
            part[j, 1] = _dot(xc[0], wub2[s], 1, 0)
            part[j, 2] = _dot(xc[1], wdb2[s], 1, 1)

        @pl.when((rest >= 2) & (rest < nrest + 2))
        def _():
            for c in k_copies(rest - 2):
                c.start()

        @pl.when((rest >= 1) & (rest < nrest + 1))
        def _():
            r = rest - 1
            j = nfull + r
            d_copy(j).wait_recv()
            for k in range(3):
                give[r, k] = part[j, k, pl.ds(away_abs, 32), :] + rdat[j, k, pl.ds(away, 32), :]
                keep[r, k] = part[j, k, pl.ds(own_abs, 32), :] + rdat[j, k, pl.ds(own, 32), :]

        @pl.when((rest >= 0) & (rest < nrest))
        def _():
            d_copy(nfull + rest).start()

        @pl.when((i >= KD) & (i < nfull + KD))
        def _():
            g_copy(i - KD).wait_recv()
            f_copy(i - KD).start()

        @pl.when((i >= KC) & (i < nfull + KC))
        def _():
            j = i - KC
            x_copy(j).wait_recv()
            vals = [part[j, k, pl.ds(own_abs, 32), :] + rdat[j, k, pl.ds(own, 32), :] + rx[j, k]
                    for k in range(3)]
            for k, v in enumerate(_sigmoid_parts(*vals)):
                hdd[j, k, pl.ds(own_abs, 32), :] = v

        return carry

    lax.fori_loop(0, nfull + KE, step, 0)

    cc = pltpu.make_async_copy(xc, xc_out, csem)
    cc.start()

    def finish_full(j, carry):
        x_copy(j).wait_send()
        g_copy(j).wait_send()
        f_copy(j).wait_send()
        o_copy(j).wait()
        return carry

    def finish_all(j, carry):
        d_copy(j).wait_send()
        return carry

    def finish_rest(r, carry):
        for c in k_copies(r):
            c.wait()
        return carry

    lax.fori_loop(0, nfull, finish_full, 0)
    lax.fori_loop(0, nch, finish_all, 0)
    lax.fori_loop(0, nrest, finish_rest, 0)
    cc.wait()


def _exchange(x_loc, gy_loc, wg, wu, wd, nfull):
    dd, ff = wg.shape
    nch = ff // CW
    nrest = nch - nfull
    tok = 128
    vm = pl.BlockSpec(memory_space=pltpu.VMEM)
    hbm = pl.BlockSpec(memory_space=pl.ANY)
    dma = pltpu.SemaphoreType.DMA
    return pl.pallas_call(
        functools.partial(_exchange_kernel, nch, nfull),
        out_shape=(jax.ShapeDtypeStruct((2, tok, dd), F32),
                   jax.ShapeDtypeStruct((2, tok, dd), BF16),
                   jax.ShapeDtypeStruct((nfull, 3, tok, CW), BF16),
                   jax.ShapeDtypeStruct((nrest, 3, 32, CW), F32),
                   jax.ShapeDtypeStruct((nrest, 3, 32, CW), F32)),
        in_specs=[vm, vm, hbm, hbm, hbm],
        out_specs=(vm, hbm, hbm, hbm, hbm),
        scratch_shapes=[
            pltpu.VMEM((2, tok, dd), BF16),
            pltpu.VMEM((SLOTS, dd, CW), BF16),
            pltpu.VMEM((SLOTS, dd, CW), BF16),
            pltpu.VMEM((SLOTS, CW, dd), BF16),
            pltpu.VMEM((SLOTS2, dd, CW), BF16),
            pltpu.VMEM((SLOTS2, dd, CW), BF16),
            pltpu.VMEM((SLOTS2, CW, dd), BF16),
            pltpu.VMEM((nch, 3, tok, CW), F32),
            pltpu.VMEM((nch, 3, 64, CW), F32),
            pltpu.VMEM((nfull, 3, 32, CW), F32),
            pltpu.VMEM((nfull, 3, 32, CW), F32),
            pltpu.VMEM((nfull, 3, tok, CW), BF16),
            pltpu.VMEM((nrest, 3, 32, CW), F32),
            pltpu.VMEM((nrest, 3, 32, CW), F32),
            dma((3, SLOTS)), dma((3, SLOTS2)), dma((2, 7)), dma((2, 7)),
            dma((nch,)), dma((nch,)), dma((nfull,)), dma((nfull,)),
            dma((nfull,)), dma((nfull,)), dma((nfull,)), dma((nfull,)),
            dma((nfull,)), dma(()), dma((2, nrest)),
        ],
        compiler_params=pltpu.CompilerParams(
            collective_id=0, has_side_effects=True, vmem_limit_bytes=66 * 1000 * 1000),
        cost_estimate=pl.CostEstimate(flops=12 * tok * dd * ff, bytes_accessed=6 * dd * ff,
                                      transcendentals=0),
        name="exchange",
    )(x_loc, gy_loc, wg, wu, wd)


def _finish_kernel(nfull, nrest, acc_in, keep, got, wg_ref, wu_ref, wd_ref,
                   give, hdd_out, acc, wgb, wub, wdb, hdd,
                   wsem, gs, gr, fs, fr, osem):
    dp = lax.axis_index("dp")
    xi = dp // 2
    co = dp % 2
    mine = pl.multiple_of(co * 64, 64)
    own_abs = pl.multiple_of(co * 64 + xi * 32, 32)
    partner = {"dp": xi * 2 + (1 - co)}
    xpeer = {"dp": (1 - xi) * 2 + co}

    def wcopies(r):
        cols = pl.ds(pl.multiple_of((nfull + r) * CW, CW), CW)
        return (pltpu.make_async_copy(wg_ref.at[:, cols], wgb.at[r], wsem.at[0, r]),
                pltpu.make_async_copy(wu_ref.at[:, cols], wub.at[r], wsem.at[1, r]),
                pltpu.make_async_copy(wd_ref.at[cols, :], wdb.at[r], wsem.at[2, r]))

    def g_copy(r):
        blk = hdd.at[r, :, pl.ds(own_abs, 32), :]
        return _remote(blk, blk, gs.at[r], gr.at[r], xpeer)

    def f_copy(r):
        blk = hdd.at[r, :, pl.ds(mine, 64), :]
        return _remote(blk, blk, fs.at[r], fr.at[r], partner)

    def o_copy(r):
        return pltpu.make_async_copy(hdd.at[r], hdd_out.at[r], osem.at[r])

    barrier = pltpu.get_barrier_semaphore()
    for dev in (partner, xpeer):
        pl.semaphore_signal(barrier, inc=1, device_id=dev, device_id_type=pl.DeviceIdType.MESH)

    def fetch(r, carry):
        for c in wcopies(r):
            c.start()
        return carry

    lax.fori_loop(0, nrest, fetch, 0)
    acc[...] = acc_in[...]
    pl.semaphore_wait(barrier, 2)

    def point(r, carry):
        @pl.when(r < nrest)
        def _():
            vals = [keep[r, k] + got[r, k] for k in range(3)]
            for k, v in enumerate(_sigmoid_parts(*vals)):
                hdd[r, k, pl.ds(own_abs, 32), :] = v

        @pl.when(r >= 1)
        def _():
            g_copy(r - 1).start()

        return carry

    lax.fori_loop(0, nrest + 1, point, 0)

    def step(i, carry):
        @pl.when(i < nrest)
        def _():
            g_copy(i).wait_recv()
            f_copy(i).start()

        @pl.when(i >= 1)
        def _():
            r = i - 1
            for c in wcopies(r):
                c.wait()
            f_copy(r).wait_recv()
            o_copy(r).start()
            acc[0] += _dot(hdd[r, 0], wdb[r], 1, 0)
            acc[1] += _dot(hdd[r, 1], wgb[r], 1, 1) + _dot(hdd[r, 2], wub[r], 1, 1)

        return carry

    lax.fori_loop(0, nrest + 1, step, 0)

    for t in range(2):
        for q in range(4):
            row = (q % 2) * 64 + (q // 2) * 32 + t * 16
            give[t * 4 + q] = acc[:, row:row + 16, :]

    def finish(r, carry):
        g_copy(r).wait_send()
        f_copy(r).wait_send()
        o_copy(r).wait()
        return carry

    lax.fori_loop(0, nrest, finish, 0)


def _finish(acc, keep, got, wg, wu, wd):
    dd, ff = wg.shape
    nrest = keep.shape[0]
    nfull = ff // CW - nrest
    tok = acc.shape[1]
    vm = pl.BlockSpec(memory_space=pltpu.VMEM)
    hbm = pl.BlockSpec(memory_space=pl.ANY)
    dma = pltpu.SemaphoreType.DMA
    return pl.pallas_call(
        functools.partial(_finish_kernel, nfull, nrest),
        out_shape=(jax.ShapeDtypeStruct((8, 2, 16, dd), F32),
                   jax.ShapeDtypeStruct((nrest, 3, tok, CW), BF16)),
        in_specs=[vm, vm, vm, hbm, hbm, hbm],
        out_specs=(vm, hbm),
        scratch_shapes=[
            pltpu.VMEM((2, tok, dd), F32),
            pltpu.VMEM((nrest, dd, CW), BF16),
            pltpu.VMEM((nrest, dd, CW), BF16),
            pltpu.VMEM((nrest, CW, dd), BF16),
            pltpu.VMEM((nrest, 3, tok, CW), BF16),
            dma((3, nrest)), dma((nrest,)), dma((nrest,)), dma((nrest,)), dma((nrest,)),
            dma((nrest,)),
        ],
        compiler_params=pltpu.CompilerParams(
            collective_id=1, has_side_effects=True, vmem_limit_bytes=60 * 1000 * 1000),
        cost_estimate=pl.CostEstimate(flops=6 * tok * dd * nrest * CW, bytes_accessed=6 * dd * nrest * CW,
                                      transcendentals=0),
        name="finish",
    )(acc, keep, got, wg, wu, wd)


def _grads_kernel(base, nch, xc_ref, hdd_ref, *refs):
    gwg_ref, gwu_ref, gwd_ref, hdd, xt, og, ou, od, isem, osem = refs[-10:]

    def fetch(j):
        return pltpu.make_async_copy(hdd_ref.at[j], hdd.at[j], isem.at[j])

    def put(j):
        s = j % RING
        cols = pl.ds(pl.multiple_of((base + j) * CW, CW), CW)
        return (pltpu.make_async_copy(og.at[s], gwg_ref.at[:, cols], osem.at[0, s]),
                pltpu.make_async_copy(ou.at[s], gwu_ref.at[:, cols], osem.at[1, s]),
                pltpu.make_async_copy(od.at[s], gwd_ref.at[cols, :], osem.at[2, s]))

    def start_fetch(j, carry):
        fetch(j).start()
        return carry

    lax.fori_loop(0, nch, start_fetch, 0)
    xt[...] = xc_ref[0].T

    def step(j, carry):
        s = j % RING

        @pl.when(j >= RING)
        def _():
            for c in put(j - RING):
                c.wait()

        fetch(j).wait()
        og[s] = _dot(xt[...], hdd[j, 1], 1, 0)
        ou[s] = _dot(xt[...], hdd[j, 2], 1, 0)
        od[s] = _dot(hdd[j, 0], xc_ref[1], 0, 0)
        for c in put(j):
            c.start()
        return carry

    lax.fori_loop(0, nch, step, 0)

    def drain(j, carry):
        for c in put(j):
            c.wait()
        return carry

    lax.fori_loop(nch - RING, nch, drain, 0)


def _grads(xc, hdd, base, ff, out=()):
    nch = hdd.shape[0]
    _, tok, dd = xc.shape
    hbm = pl.BlockSpec(memory_space=pl.ANY)
    dma = pltpu.SemaphoreType.DMA
    return pl.pallas_call(
        functools.partial(_grads_kernel, base, nch),
        out_shape=(jax.ShapeDtypeStruct((dd, ff), F32), jax.ShapeDtypeStruct((dd, ff), F32),
                   jax.ShapeDtypeStruct((ff, dd), F32)),
        in_specs=[pl.BlockSpec(memory_space=pltpu.VMEM), hbm] + [hbm] * len(out),
        out_specs=(hbm, hbm, hbm),
        input_output_aliases={2 + n: n for n in range(len(out))},
        scratch_shapes=[
            pltpu.VMEM(hdd.shape, BF16), pltpu.VMEM((dd, tok), BF16),
            pltpu.VMEM((RING, dd, CW), F32), pltpu.VMEM((RING, dd, CW), F32),
            pltpu.VMEM((RING, CW, dd), F32),
            dma((nch,)), dma((3, RING)),
        ],
        compiler_params=pltpu.CompilerParams(vmem_limit_bytes=GRAD_VMEM),
        cost_estimate=pl.CostEstimate(flops=6 * tok * dd * nch * CW, bytes_accessed=12 * dd * nch * CW,
                                      transcendentals=0),
        name="grads",
    )(xc, hdd, *out)


def solution(mesh):
    def local_step(x_loc, wg, wu, wd, gy_loc):
        ff = wg.shape[1]
        acc, xc, hdd, give, keep = _exchange(x_loc, gy_loc, wg, wu, wd, NFULL)
        got = lax.ppermute(give, "dp", [(0, 2), (1, 3), (2, 0), (3, 1)])
        grads = _grads(xc, hdd, 0, ff)
        grads, keep = lax.optimization_barrier((grads, keep))
        give, hdd = _finish(acc, keep, got, wg, wu, wd)
        got = lax.all_to_all(give, ("tp", "dp"), 0, 0, tiled=True)
        gwg, gwu, gwd = _grads(xc, hdd, NFULL, ff, grads)

        def own_rows(k, resid):
            both = [got[q, k] + got[q + 4, k] for q in range(4)]
            return (jnp.concatenate(both, axis=1) + resid.astype(F32)).astype(BF16)

        return own_rows(0, x_loc), own_rows(1, gy_loc), gwg, gwu, gwd

    row_spec = P(("dp", "tp"), None)
    up_spec = P("dp", "tp")
    down_spec = P("tp", "dp")
    return jax.shard_map(local_step, mesh=mesh,
                         in_specs=(row_spec, up_spec, up_spec, down_spec, row_spec),
                         out_specs=(row_spec, row_spec, up_spec, up_spec, down_spec),
                         check_vma=False)
```

time: 181 us -> 171 us (0.945)
  Pallas kernels: 176 us -> 163 us
    pallas_call x2 -> x4, Pallas kernels: 176 us -> 163 us  [the longest x1 106 us: _exchange(): pl.pallas_call(functools.partial(_exchange_kernel, nch, nfull), out_shape...]
  transfers between devices with their start and end apart: 1 -> 2, of which waited for: 0 -> 1; matrix products, arithmetic and copies ran while one was open for 0% -> 0% of each run, Pallas kernels for 19% -> 22%
where the time goes in v3:
time: 171 us; the launch traced here: 170 us
  Pallas kernels  163 us (95%)
  starting transfers between devices  3.33 us (2%)
    pallas_call x1, Pallas kernels, _exchange(): pl.pallas_call(functools.partial(_exchange_kernel, nch, nfull), out_shape...  106 us
    pallas_call x2, Pallas kernels, _grads(): pl.pallas_call(functools.partial(_grads_kernel, base, nch), out_shape=(ja...  37.6 us
    pallas_call x1, Pallas kernels, _finish(): pl.pallas_call(functools.partial(_finish_kernel, nfull, nrest), out_shape...  19.9 us
  transfers between devices with their start and end apart: 2, of which 1 were waited for; matrix products, arithmetic and copies ran while one was open for 0% of the time, Pallas kernels for 22%

profile of v3, /device:TPU:0, one launch (start us, length us, event | category | flops | bytes accessed | tf_op | source)
XLA Modules:
  0.0 170.5 jit_solution(10086761010763663542)
XLA Ops:
  0.6 106.0 %exchange.1 = (f32[2,128,896]{2,1,0:T(8,128)}, bf16[2,128,896]{2,1,0:T(8,128)(2,1)}, bf16[26,3,128,256]{3,2,1,0:T(8,128)(2,1)}, f32[11,3,32,256]{3,2,1,0:T(8,128)}, f32[11,3,32,256]{3,2,1,0:T(8,128)}) custom-call(bf16[16,3584]{1,0:T(8,128)(2,1)} %x_ref.1, bf16[16,3584]{1,0:T(8,128)(2,1)} %gy_ref.1, bf16[896,9472]{1,0:T(8,128)(2,1)} %wg_ref.3, ...), custom_call_target="tpu_custom_call" | custom-call | flops 13035896832 | bytes 50921472 | tf_op jit(solution)/shard_map/exchange/pallas_call | solution.py:264
  106.6 1.0 collective-permute-start
  107.7 25.0 %grads.2 = (f32[896,9472]{1,0:T(8,128)}, f32[896,9472]{1,0:T(8,128)}, f32[9472,896]{1,0:T(8,128)}) custom-call(bf16[2,128,896]{2,1,0:T(8,128)(2,1)} %get-tuple-element.23.xc_ref, bf16[26,3,128,256]{3,2,1,0:T(8,128)(2,1)} %get-tuple-element.24.hdd_ref), custom_call_target="tpu_custom_call" | custom-call | flops 4580179968 | bytes 71565312 | tf_op jit(solution)/shard_map/grads/pallas_call | solution.py:473
  132.7 0.0 collective-permute-done.got
  132.7 19.9 %finish.1 = (f32[8,2,16,896]{3,2,1,0:T(8,128)}, bf16[11,3,128,256]{3,2,1,0:T(8,128)(2,1)}) custom-call(f32[2,128,896]{2,1,0:T(8,128)} %get-tuple-element.22.acc_in, f32[11,3,32,256]{3,2,1,0:T(8,128)} %get-tuple-element.29.keep, f32[11,3,32,256]{3,2,1,0:T(8,128)} %collective-permute-done.got, bf16[896,9472]{1,0:T(8,128)(2,1)} %wg_ref.3, ...), custom_call_target="tpu_custom_call" | custom-call | flops 1937768448 | bytes 15138816 | tf_op jit(solution)/shard_map/finish/pallas_call | solution.py:399
  152.6 2.3 %all-to-all-start = ((f32[8,2,16,896]{3,2,1,0:T(8,128)}), f32[8,2,16,896]{3,2,1,0:T(8,128)S(1)}, u32[]{:S(2)}, u32[]{:S(2)}) async-start(f32[8,2,16,896]{3,2,1,0:T(8,128)} %get-tuple-element.31), calls=%async_computation | async-start | bytes 1835008 | tf_op jit(solution)/shard_map/all_to_all | solution.py:501
  154.9 0.0 copy-start
  154.9 12.5 %grads.3 = (f32[896,9472]{1,0:T(8,128)}, f32[896,9472]{1,0:T(8,128)}, f32[9472,896]{1,0:T(8,128)}) custom-call(bf16[2,128,896]{2,1,0:T(8,128)(2,1)} %get-tuple-element.23.xc_ref, bf16[11,3,128,256]{3,2,1,0:T(8,128)(2,1)} %get-tuple-element.32.hdd_ref, ...), custom_call_target="tpu_custom_call", output_to_operand_aliasing={{0}: (2, {}), {1}: (3, {}), {2}: (4, {})} | custom-call | flops 1937768448 | bytes 30277632 | tf_op jit(solution)/shard_map/grads/pallas_call | solution.py:473
  167.5 1.3 all-to-all-done
  168.8 0.0 copy-done
  168.8 1.6 fusion
  (1 shorter events, 0.0 us)
Async XLA Ops:
  106.6 26.1 %collective-permute-start = (f32[11,3,32,256]{3,2,1,0:T(8,128)}, f32[11,3,32,256]{3,2,1,0:T(8,128)}, u32[]{:S(2)}, u32[]{:S(2)}) collective-permute-start(f32[11,3,32,256]{3,2,1,0:T(8,128)} %get-tuple-element.30), channel_id=1, source_target_pairs={{0,2},{1,3},{2,0},{3,1},{4,6},{5,7},{6,4},{7,5}} | collective-permute-start | bytes 3244040 | tf_op jit(solution)/shard_map/ppermute | solution.py:497
  152.6 16.2 %all-to-all-start = ((f32[8,2,16,896]{3,2,1,0:T(8,128)}), f32[8,2,16,896]{3,2,1,0:T(8,128)S(1)}, u32[]{:S(2)}, u32[]{:S(2)}) async-start(f32[8,2,16,896]{3,2,1,0:T(8,128)} %get-tuple-element.31), calls=%async_computation | async-start | bytes 1835008 | tf_op jit(solution)/shard_map/all_to_all | solution.py:501
  154.9 13.9 %copy-start = (bf16[16,3584]{1,0:T(8,128)(2,1)S(1)}, bf16[16,3584]{1,0:T(8,128)(2,1)}, u32[]{:S(2)}) copy-start(bf16[16,3584]{1,0:T(8,128)(2,1)} %x_ref.1) | copy-start | bytes 344068

commit v4 on v3

--- a/solution.py
+++ b/solution.py
@@ -40,7 +40,7 @@
 def _exchange_kernel(nch, nfull, x_ref, gy_ref, wg_ref, wu_ref, wd_ref,
                      acc, xc_out, hdd_out, give_out, keep_out,
                      xc, wgb, wub, wdb, wgb2, wub2, wdb2, part, rdat, sx, rx, hdd, give, keep,
-                     wsem, wsem2, tsem_s, tsem_r, ds, dr, xs, xr, gs, gr, fs, fr, osem, csem, ksem):
+                     wsem, wsem2, tsem_s, tsem_r, ds, dr, xs, xr, gs, gr, fs, fr, osem, csem, ksem, absem):
     nrest = nch - nfull
     dp = lax.axis_index("dp")
     tp = lax.axis_index("tp")
@@ -68,7 +68,7 @@
     def rest_w(r):
         return wcopies(nfull + r, r % SLOTS2, (wgb2, wub2, wdb2), wsem2)
 
-    for j in range(AHEAD):
+    for j in range(AHEAD + 1):
         for c in first_w(j):
             c.start()
 
@@ -126,6 +126,25 @@
         return (pltpu.make_async_copy(give.at[r], give_out.at[r], ksem.at[0, r]),
                 pltpu.make_async_copy(keep.at[r], keep_out.at[r], ksem.at[1, r]))
 
+    def sum_away(j, k):
+        return part[j, k, pl.ds(away_abs, 32), :] + rdat[j, k, pl.ds(away, 32), :]
+
+    for c in first_w(0):
+        c.wait()
+    part[0, 0] = _dot(xc[0], wgb[0], 1, 0)
+    part[0, 1] = _dot(xc[0], wub[0], 1, 0)
+    d_ab = _remote(part.at[0, 0:2, pl.ds(other, 64), :], rdat.at[0, 0:2], ds.at[0], absem, partner)
+    d_ab.start()
+    d_ab.wait_recv()
+    sx[0, 0] = sum_away(0, 0)
+    sx[0, 1] = sum_away(0, 1)
+    _remote(sx.at[0, 0:2], rx.at[0, 0:2], xs.at[0], xr.at[0], xpeer).start()
+    for c in tok[len(rel):]:
+        c.wait()
+    part[0, 2] = _dot(xc[1], wdb[0], 1, 1)
+    d_g = _remote(part.at[0, 2:3, pl.ds(other, 64), :], rdat.at[0, 2:3], ds.at[0], dr.at[0], partner)
+    d_g.start()
+
     def step(i, carry):
         rest = i - REST_AT
 
@@ -147,23 +166,24 @@
             part[i, 0] = _dot(xc[0], wgb[s], 1, 0)
             part[i, 1] = _dot(xc[0], wub[s], 1, 0)
 
-            @pl.when(i == 0)
-            def _():
-                for c in tok[len(rel):]:
-                    c.wait()
-
             part[i, 2] = _dot(xc[1], wdb[s], 1, 1)
 
         @pl.when((i >= KC + 1) & (i < nfull + KC + 1))
         def _():
             g_copy(i - KC - 1).start()
 
-        @pl.when((i >= 1) & (i < nfull + 1))
+        @pl.when(i == 1)
+        def _():
+            d_g.wait_recv()
+            sx[0, 2] = sum_away(0, 2)
+            _remote(sx.at[0, 2:3], rx.at[0, 2:3], xs.at[0], xr.at[0], xpeer).start()
+
+        @pl.when((i >= 2) & (i < nfull + 1))
         def _():
             j = i - 1
             d_copy(j).wait_recv()
             for k in range(3):
-                sx[j, k] = part[j, k, pl.ds(away_abs, 32), :] + rdat[j, k, pl.ds(away, 32), :]
+                sx[j, k] = sum_away(j, k)
 
         @pl.when(i < nfull)
         def _():
@@ -178,7 +198,7 @@
             acc[0] += _dot(hdd[j, 0], wdb[s], 1, 0)
             acc[1] += _dot(hdd[j, 1], wgb[s], 1, 1) + _dot(hdd[j, 2], wub[s], 1, 1)
 
-        @pl.when((i >= 1) & (i < nfull + 1))
+        @pl.when((i >= 2) & (i < nfull + 1))
         def _():
             x_copy(i - 1).start()
 
@@ -203,7 +223,7 @@
             j = nfull + r
             d_copy(j).wait_recv()
             for k in range(3):
-                give[r, k] = part[j, k, pl.ds(away_abs, 32), :] + rdat[j, k, pl.ds(away, 32), :]
+                give[r, k] = sum_away(j, k)
                 keep[r, k] = part[j, k, pl.ds(own_abs, 32), :] + rdat[j, k, pl.ds(own, 32), :]
 
         @pl.when((rest >= 0) & (rest < nrest))
@@ -226,7 +246,7 @@
 
         return carry
 
-    lax.fori_loop(0, nfull + KE, step, 0)
+    lax.fori_loop(1, nfull + KE, step, 0)
 
     cc = pltpu.make_async_copy(xc, xc_out, csem)
     cc.start()
@@ -288,7 +308,7 @@
             dma((3, SLOTS)), dma((3, SLOTS2)), dma((2, 7)), dma((2, 7)),
             dma((nch,)), dma((nch,)), dma((nfull,)), dma((nfull,)),
             dma((nfull,)), dma((nfull,)), dma((nfull,)), dma((nfull,)),
-            dma((nfull,)), dma(()), dma((2, nrest)),
+            dma((nfull,)), dma(()), dma((2, nrest)), dma(()),
         ],
         compiler_params=pltpu.CompilerParams(
             collective_id=0, has_side_effects=True, vmem_limit_bytes=66 * 1000 * 1000),
@@ -298,9 +318,9 @@
     )(x_loc, gy_loc, wg, wu, wd)
 
 
-def _finish_kernel(nfull, nrest, acc_in, keep, got, wg_ref, wu_ref, wd_ref,
-                   give, hdd_out, acc, wgb, wub, wdb, hdd,
-                   wsem, gs, gr, fs, fr, osem):
+def _finish_kernel(nfull, nrest, acc_in, keep_ref, got_ref, wg_ref, wu_ref, wd_ref,
+                   give, hdd_out, acc, keep, got, wgb, wub, wdb, hdd,
+                   wsem, isem, asem, gs, gr, fs, fr, osem):
     dp = lax.axis_index("dp")
     xi = dp // 2
     co = dp % 2
@@ -335,13 +355,26 @@
             c.start()
         return carry
 
+    def icopies(r):
+        return (pltpu.make_async_copy(keep_ref.at[r], keep.at[r], isem.at[0, r]),
+                pltpu.make_async_copy(got_ref.at[r], got.at[r], isem.at[1, r]))
+
+    def fetch_sums(r, carry):
+        for c in icopies(r):
+            c.start()
+        return carry
+
+    lax.fori_loop(0, nrest, fetch_sums, 0)
+    acopy = pltpu.make_async_copy(acc_in, acc, asem)
+    acopy.start()
     lax.fori_loop(0, nrest, fetch, 0)
-    acc[...] = acc_in[...]
     pl.semaphore_wait(barrier, 2)
 
     def point(r, carry):
         @pl.when(r < nrest)
         def _():
+            for c in icopies(r):
+                c.wait()
             vals = [keep[r, k] + got[r, k] for k in range(3)]
             for k, v in enumerate(_sigmoid_parts(*vals)):
                 hdd[r, k, pl.ds(own_abs, 32), :] = v
@@ -353,6 +386,7 @@
         return carry
 
     lax.fori_loop(0, nrest + 1, point, 0)
+    acopy.wait()
 
     def step(i, carry):
         @pl.when(i < nrest)
@@ -400,19 +434,21 @@
         functools.partial(_finish_kernel, nfull, nrest),
         out_shape=(jax.ShapeDtypeStruct((8, 2, 16, dd), F32),
                    jax.ShapeDtypeStruct((nrest, 3, tok, CW), BF16)),
-        in_specs=[vm, vm, vm, hbm, hbm, hbm],
+        in_specs=[hbm] * 6,
         out_specs=(vm, hbm),
         scratch_shapes=[
             pltpu.VMEM((2, tok, dd), F32),
+            pltpu.VMEM((nrest, 3, 32, CW), F32),
+            pltpu.VMEM((nrest, 3, 32, CW), F32),
             pltpu.VMEM((nrest, dd, CW), BF16),
             pltpu.VMEM((nrest, dd, CW), BF16),
             pltpu.VMEM((nrest, CW, dd), BF16),
             pltpu.VMEM((nrest, 3, tok, CW), BF16),
-            dma((3, nrest)), dma((nrest,)), dma((nrest,)), dma((nrest,)), dma((nrest,)),
+            dma((3, nrest)), dma((2, nrest)), dma(()), dma((nrest,)), dma((nrest,)), dma((nrest,)), dma((nrest,)),
             dma((nrest,)),
         ],
         compiler_params=pltpu.CompilerParams(
-            collective_id=1, has_side_effects=True, vmem_limit_bytes=60 * 1000 * 1000),
+            collective_id=1, has_side_effects=True, vmem_limit_bytes=66 * 1000 * 1000),
         cost_estimate=pl.CostEstimate(flops=6 * tok * dd * nrest * CW, bytes_accessed=6 * dd * nrest * CW,
                                       transcendentals=0),
         name="finish",
@@ -420,7 +456,7 @@
 
 
 def _grads_kernel(base, nch, xc_ref, hdd_ref, *refs):
-    gwg_ref, gwu_ref, gwd_ref, hdd, xt, og, ou, od, isem, osem = refs[-10:]
+    gwg_ref, gwu_ref, gwd_ref, hdd, xc, xt, og, ou, od, isem, osem, csem = refs[-12:]
 
     def fetch(j):
         return pltpu.make_async_copy(hdd_ref.at[j], hdd.at[j], isem.at[j])
@@ -436,8 +472,11 @@
         fetch(j).start()
         return carry
 
+    ccopy = pltpu.make_async_copy(xc_ref, xc, csem)
+    ccopy.start()
     lax.fori_loop(0, nch, start_fetch, 0)
-    xt[...] = xc_ref[0].T
+    ccopy.wait()
+    xt[...] = xc[0].T
 
     def step(j, carry):
         s = j % RING
@@ -450,7 +489,7 @@
         fetch(j).wait()
         og[s] = _dot(xt[...], hdd[j, 1], 1, 0)
         ou[s] = _dot(xt[...], hdd[j, 2], 1, 0)
-        od[s] = _dot(hdd[j, 0], xc_ref[1], 0, 0)
+        od[s] = _dot(hdd[j, 0], xc[1], 0, 0)
         for c in put(j):
             c.start()
         return carry
@@ -474,14 +513,14 @@
         functools.partial(_grads_kernel, base, nch),
         out_shape=(jax.ShapeDtypeStruct((dd, ff), F32), jax.ShapeDtypeStruct((dd, ff), F32),
                    jax.ShapeDtypeStruct((ff, dd), F32)),
-        in_specs=[pl.BlockSpec(memory_space=pltpu.VMEM), hbm] + [hbm] * len(out),
+        in_specs=[hbm] * (2 + len(out)),
         out_specs=(hbm, hbm, hbm),
         input_output_aliases={2 + n: n for n in range(len(out))},
         scratch_shapes=[
-            pltpu.VMEM(hdd.shape, BF16), pltpu.VMEM((dd, tok), BF16),
+            pltpu.VMEM(hdd.shape, BF16), pltpu.VMEM(xc.shape, BF16), pltpu.VMEM((dd, tok), BF16),
             pltpu.VMEM((RING, dd, CW), F32), pltpu.VMEM((RING, dd, CW), F32),
             pltpu.VMEM((RING, CW, dd), F32),
-            dma((nch,)), dma((3, RING)),
+            dma((nch,)), dma((3, RING)), dma(()),
         ],
         compiler_params=pltpu.CompilerParams(vmem_limit_bytes=GRAD_VMEM),
         cost_estimate=pl.CostEstimate(flops=6 * tok * dd * nch * CW, bytes_accessed=12 * dd * nch * CW,

time: 171 us -> 167 us (0.977)
  Pallas kernels: 163 us -> 159 us
where the time goes in v4:
time: 167 us
  Pallas kernels  159 us (95%)
  starting transfers between devices  3.33 us (2%)
  waiting for transfers between devices  2.13 us (1%)
  other arithmetic  1.69 us (1%)
    pallas_call x1, Pallas kernels, _exchange(): pl.pallas_call(functools.partial(_exchange_kernel, nch, nfull), out_shape...  105 us
    pallas_call x2, Pallas kernels, _grads(): pl.pallas_call(functools.partial(_grads_kernel, base, nch), out_shape=(ja...  36 us
    pallas_call x1, Pallas kernels, _finish(): pl.pallas_call(functools.partial(_finish_kernel, nfull, nrest), out_shape...  18.4 us
  transfers between devices with their start and end apart: 2, of which 1 were waited for; matrix products, arithmetic and copies ran while one was open for 0% of the time, Pallas kernels for 22%

profile of v4, /device:TPU:0, one launch (start us, length us, event | category | flops | bytes accessed | tf_op | source)
XLA Modules:
  0.0 167.1 jit_solution(11708180284008201519)
XLA Ops:
  0.6 104.8 %exchange.1 = (f32[2,128,896]{2,1,0:T(8,128)}, bf16[2,128,896]{2,1,0:T(8,128)(2,1)}, bf16[26,3,128,256]{3,2,1,0:T(8,128)(2,1)}, f32[11,3,32,256]{3,2,1,0:T(8,128)}, f32[11,3,32,256]{3,2,1,0:T(8,128)}) custom-call(bf16[16,3584]{1,0:T(8,128)(2,1)} %x_ref.1, bf16[16,3584]{1,0:T(8,128)(2,1)} %gy_ref.1, bf16[896,9472]{1,0:T(8,128)(2,1)} %wg_ref.3, ...), custom_call_target="tpu_custom_call" | custom-call | flops 13035896832 | bytes 50921472 | tf_op jit(solution)/shard_map/exchange/pallas_call | solution.py:284
  105.4 1.0 collective-permute-start
  106.5 24.3 %grads.2 = (f32[896,9472]{1,0:T(8,128)}, f32[896,9472]{1,0:T(8,128)}, f32[9472,896]{1,0:T(8,128)}) custom-call(bf16[2,128,896]{2,1,0:T(8,128)(2,1)} %get-tuple-element.23.xc_ref, bf16[26,3,128,256]{3,2,1,0:T(8,128)(2,1)} %get-tuple-element.24.hdd_ref), custom_call_target="tpu_custom_call" | custom-call | flops 4580179968 | bytes 71565312 | tf_op jit(solution)/shard_map/grads/pallas_call | solution.py:512
  130.7 0.0 collective-permute-done.got_ref
  130.8 18.4 %finish.1 = (f32[8,2,16,896]{3,2,1,0:T(8,128)}, bf16[11,3,128,256]{3,2,1,0:T(8,128)(2,1)}) custom-call(f32[2,128,896]{2,1,0:T(8,128)} %get-tuple-element.22.acc_in, f32[11,3,32,256]{3,2,1,0:T(8,128)} %get-tuple-element.29.keep_ref, f32[11,3,32,256]{3,2,1,0:T(8,128)} %collective-permute-done.got_ref, bf16[896,9472]{1,0:T(8,128)(2,1)} %wg_ref.3, ...), custom_call_target="tpu_custom_call" | custom-call | flops 1937768448 | bytes 15138816 | tf_op jit(solution)/shard_map/finish/pallas_call | solution.py:433
  149.2 2.3 %all-to-all-start = ((f32[8,2,16,896]{3,2,1,0:T(8,128)}), f32[8,2,16,896]{3,2,1,0:T(8,128)S(1)}, u32[]{:S(2)}, u32[]{:S(2)}) async-start(f32[8,2,16,896]{3,2,1,0:T(8,128)} %get-tuple-element.31), calls=%async_computation | async-start | bytes 1835008 | tf_op jit(solution)/shard_map/all_to_all | solution.py:540
  151.5 0.0 copy-start
  151.5 11.7 %grads.3 = (f32[896,9472]{1,0:T(8,128)}, f32[896,9472]{1,0:T(8,128)}, f32[9472,896]{1,0:T(8,128)}) custom-call(bf16[2,128,896]{2,1,0:T(8,128)(2,1)} %get-tuple-element.23.xc_ref, bf16[11,3,128,256]{3,2,1,0:T(8,128)(2,1)} %get-tuple-element.32.hdd_ref, ...), custom_call_target="tpu_custom_call", output_to_operand_aliasing={{0}: (2, {}), {1}: (3, {}), {2}: (4, {})} | custom-call | flops 1937768448 | bytes 30277632 | tf_op jit(solution)/shard_map/grads/pallas_call | solution.py:512
  163.3 2.1 %all-to-all-done = f32[8,2,16,896]{3,2,1,0:T(8,128)S(1)} async-done(((f32[8,2,16,896]{3,2,1,0:T(8,128)}), f32[8,2,16,896]{3,2,1,0:T(8,128)S(1)}, u32[]{:S(2)}, u32[]{:S(2)}) %all-to-all-start) | async-done | bytes 917536 | tf_op jit(solution)/shard_map/all_to_all | solution.py:540
  165.4 0.0 copy-done
  165.4 1.6 fusion
  (1 shorter events, 0.0 us)
Async XLA Ops:
  105.4 25.3 %collective-permute-start = (f32[11,3,32,256]{3,2,1,0:T(8,128)}, f32[11,3,32,256]{3,2,1,0:T(8,128)}, u32[]{:S(2)}, u32[]{:S(2)}) collective-permute-start(f32[11,3,32,256]{3,2,1,0:T(8,128)} %get-tuple-element.30), channel_id=1, source_target_pairs={{0,2},{1,3},{2,0},{3,1},{4,6},{5,7},{6,4},{7,5}} | collective-permute-start | bytes 3244040 | tf_op jit(solution)/shard_map/ppermute | solution.py:536
  149.2 16.2 %all-to-all-start = ((f32[8,2,16,896]{3,2,1,0:T(8,128)}), f32[8,2,16,896]{3,2,1,0:T(8,128)S(1)}, u32[]{:S(2)}, u32[]{:S(2)}) async-start(f32[8,2,16,896]{3,2,1,0:T(8,128)} %get-tuple-element.31), calls=%async_computation | async-start | bytes 1835008 | tf_op jit(solution)/shard_map/all_to_all | solution.py:540
  151.5 13.9 %copy-start = (bf16[16,3584]{1,0:T(8,128)(2,1)S(1)}, bf16[16,3584]{1,0:T(8,128)(2,1)}, u32[]{:S(2)}) copy-start(bf16[16,3584]{1,0:T(8,128)(2,1)} %x_ref.1) | copy-start | bytes 344068

commit v5 on v4

--- a/solution.py
+++ b/solution.py
@@ -10,9 +10,10 @@
 F32 = jnp.float32
 BF16 = jnp.bfloat16
 CW = 256
-NFULL = 26
+NFULL = 24
+NTAIL = 3
 REST_AT = 8
-GRAD_VMEM = 66 * 1000 * 1000
+GRAD_VMEM = 67_043_328
 SLOTS2 = 3
 AHEAD2 = 2
 SLOTS = 11
@@ -38,9 +39,10 @@
 
 
 def _exchange_kernel(nch, nfull, x_ref, gy_ref, wg_ref, wu_ref, wd_ref,
-                     acc, xc_out, hdd_out, give_out, keep_out,
+                     acc, xc_out, hdd_out, give_out, keep_out, got_out,
                      xc, wgb, wub, wdb, wgb2, wub2, wdb2, part, rdat, sx, rx, hdd, give, keep,
-                     wsem, wsem2, tsem_s, tsem_r, ds, dr, xs, xr, gs, gr, fs, fr, osem, csem, ksem, absem):
+                     wsem, wsem2, tsem_s, tsem_r, ds, dr, xs, xr, gs, gr, fs, fr, osem, csem, ksem, absem,
+                     ts, tr):
     nrest = nch - nfull
     dp = lax.axis_index("dp")
     tp = lax.axis_index("tp")
@@ -122,9 +124,14 @@
     def o_copy(j):
         return pltpu.make_async_copy(hdd.at[j], hdd_out.at[j], osem.at[j])
 
-    def k_copies(r):
-        return (pltpu.make_async_copy(give.at[r], give_out.at[r], ksem.at[0, r]),
-                pltpu.make_async_copy(keep.at[r], keep_out.at[r], ksem.at[1, r]))
+    def give_copy(r):
+        return pltpu.make_async_copy(give.at[r], give_out.at[r - NTAIL], ksem.at[0, r])
+
+    def keep_copy(r):
+        return pltpu.make_async_copy(keep.at[r], keep_out.at[r], ksem.at[1, r])
+
+    def t_copy(r):
+        return _remote(give.at[r], got_out.at[r], ts.at[r], tr.at[r], xpeer)
 
     def sum_away(j, k):
         return part[j, k, pl.ds(away_abs, 32), :] + rdat[j, k, pl.ds(away, 32), :]
@@ -172,6 +179,11 @@
         def _():
             g_copy(i - KC - 1).start()
 
+        @pl.when(i == nfull + KC)
+        def _():
+            for r in range(NTAIL):
+                t_copy(r).start()
+
         @pl.when(i == 1)
         def _():
             d_g.wait_recv()
@@ -214,8 +226,11 @@
 
         @pl.when((rest >= 2) & (rest < nrest + 2))
         def _():
-            for c in k_copies(rest - 2):
-                c.start()
+            keep_copy(rest - 2).start()
+
+        @pl.when((rest >= 2 + NTAIL) & (rest < nrest + 2))
+        def _():
+            give_copy(rest - 2).start()
 
         @pl.when((rest >= 1) & (rest < nrest + 1))
         def _():
@@ -262,14 +277,20 @@
         d_copy(j).wait_send()
         return carry
 
-    def finish_rest(r, carry):
-        for c in k_copies(r):
-            c.wait()
+    def finish_keep(r, carry):
+        keep_copy(r).wait()
+        return carry
+
+    def finish_give(r, carry):
+        give_copy(r).wait()
         return carry
 
     lax.fori_loop(0, nfull, finish_full, 0)
     lax.fori_loop(0, nch, finish_all, 0)
-    lax.fori_loop(0, nrest, finish_rest, 0)
+    lax.fori_loop(0, nrest, finish_keep, 0)
+    lax.fori_loop(NTAIL, nrest, finish_give, 0)
+    for r in range(NTAIL):
+        t_copy(r).wait()
     cc.wait()
 
 
@@ -286,10 +307,11 @@
         out_shape=(jax.ShapeDtypeStruct((2, tok, dd), F32),
                    jax.ShapeDtypeStruct((2, tok, dd), BF16),
                    jax.ShapeDtypeStruct((nfull, 3, tok, CW), BF16),
+                   jax.ShapeDtypeStruct((nrest - NTAIL, 3, 32, CW), F32),
                    jax.ShapeDtypeStruct((nrest, 3, 32, CW), F32),
-                   jax.ShapeDtypeStruct((nrest, 3, 32, CW), F32)),
+                   jax.ShapeDtypeStruct((NTAIL, 3, 32, CW), F32)),
         in_specs=[vm, vm, hbm, hbm, hbm],
-        out_specs=(vm, hbm, hbm, hbm, hbm),
+        out_specs=(vm, hbm, hbm, hbm, hbm, hbm),
         scratch_shapes=[
             pltpu.VMEM((2, tok, dd), BF16),
             pltpu.VMEM((SLOTS, dd, CW), BF16),
@@ -308,7 +330,7 @@
             dma((3, SLOTS)), dma((3, SLOTS2)), dma((2, 7)), dma((2, 7)),
             dma((nch,)), dma((nch,)), dma((nfull,)), dma((nfull,)),
             dma((nfull,)), dma((nfull,)), dma((nfull,)), dma((nfull,)),
-            dma((nfull,)), dma(()), dma((2, nrest)), dma(()),
+            dma((nfull,)), dma(()), dma((2, nrest)), dma(()), dma((NTAIL,)), dma((NTAIL,)),
         ],
         compiler_params=pltpu.CompilerParams(
             collective_id=0, has_side_effects=True, vmem_limit_bytes=66 * 1000 * 1000),
@@ -318,7 +340,7 @@
     )(x_loc, gy_loc, wg, wu, wd)
 
 
-def _finish_kernel(nfull, nrest, acc_in, keep_ref, got_ref, wg_ref, wu_ref, wd_ref,
+def _finish_kernel(nfull, nrest, acc_in, keep_ref, tail_ref, got_ref, wg_ref, wu_ref, wd_ref,
                    give, hdd_out, acc, keep, got, wgb, wub, wdb, hdd,
                    wsem, isem, asem, gs, gr, fs, fr, osem):
     dp = lax.axis_index("dp")
@@ -355,16 +377,22 @@
             c.start()
         return carry
 
-    def icopies(r):
-        return (pltpu.make_async_copy(keep_ref.at[r], keep.at[r], isem.at[0, r]),
-                pltpu.make_async_copy(got_ref.at[r], got.at[r], isem.at[1, r]))
+    def keep_in(r):
+        return pltpu.make_async_copy(keep_ref.at[r], keep.at[r], isem.at[0, r])
+
+    def got_in(r, src, at):
+        return pltpu.make_async_copy(src.at[at], got.at[r], isem.at[1, r])
+
+    for r in range(NTAIL):
+        keep_in(r).start()
+        got_in(r, tail_ref, r).start()
 
     def fetch_sums(r, carry):
-        for c in icopies(r):
-            c.start()
-        return carry
-
-    lax.fori_loop(0, nrest, fetch_sums, 0)
+        keep_in(r).start()
+        got_in(r, got_ref, r - NTAIL).start()
+        return carry
+
+    lax.fori_loop(NTAIL, nrest, fetch_sums, 0)
     acopy = pltpu.make_async_copy(acc_in, acc, asem)
     acopy.start()
     lax.fori_loop(0, nrest, fetch, 0)
@@ -373,8 +401,8 @@
     def point(r, carry):
         @pl.when(r < nrest)
         def _():
-            for c in icopies(r):
-                c.wait()
+            keep_in(r).wait()
+            got_in(r, got_ref, 0).wait()
             vals = [keep[r, k] + got[r, k] for k in range(3)]
             for k, v in enumerate(_sigmoid_parts(*vals)):
                 hdd[r, k, pl.ds(own_abs, 32), :] = v
@@ -422,7 +450,7 @@
     lax.fori_loop(0, nrest, finish, 0)
 
 
-def _finish(acc, keep, got, wg, wu, wd):
+def _finish(acc, keep, tail, got, wg, wu, wd):
     dd, ff = wg.shape
     nrest = keep.shape[0]
     nfull = ff // CW - nrest
@@ -434,7 +462,7 @@
         functools.partial(_finish_kernel, nfull, nrest),
         out_shape=(jax.ShapeDtypeStruct((8, 2, 16, dd), F32),
                    jax.ShapeDtypeStruct((nrest, 3, tok, CW), BF16)),
-        in_specs=[hbm] * 6,
+        in_specs=[hbm] * 7,
         out_specs=(vm, hbm),
         scratch_shapes=[
             pltpu.VMEM((2, tok, dd), F32),
@@ -452,7 +480,7 @@
         cost_estimate=pl.CostEstimate(flops=6 * tok * dd * nrest * CW, bytes_accessed=6 * dd * nrest * CW,
                                       transcendentals=0),
         name="finish",
-    )(acc, keep, got, wg, wu, wd)
+    )(acc, keep, tail, got, wg, wu, wd)
 
 
 def _grads_kernel(base, nch, xc_ref, hdd_ref, *refs):
@@ -522,7 +550,7 @@
             pltpu.VMEM((RING, CW, dd), F32),
             dma((nch,)), dma((3, RING)), dma(()),
         ],
-        compiler_params=pltpu.CompilerParams(vmem_limit_bytes=GRAD_VMEM),
+        compiler_params=pltpu.CompilerParams(vmem_limit_bytes=66_000_000 if out else GRAD_VMEM),
         cost_estimate=pl.CostEstimate(flops=6 * tok * dd * nch * CW, bytes_accessed=12 * dd * nch * CW,
                                       transcendentals=0),
         name="grads",
@@ -532,11 +560,11 @@
 def solution(mesh):
     def local_step(x_loc, wg, wu, wd, gy_loc):
         ff = wg.shape[1]
-        acc, xc, hdd, give, keep = _exchange(x_loc, gy_loc, wg, wu, wd, NFULL)
+        acc, xc, hdd, give, keep, tail = _exchange(x_loc, gy_loc, wg, wu, wd, NFULL)
         got = lax.ppermute(give, "dp", [(0, 2), (1, 3), (2, 0), (3, 1)])
         grads = _grads(xc, hdd, 0, ff)
         grads, keep = lax.optimization_barrier((grads, keep))
-        give, hdd = _finish(acc, keep, got, wg, wu, wd)
+        give, hdd = _finish(acc, keep, tail, got, wg, wu, wd)
         got = lax.all_to_all(give, ("tp", "dp"), 0, 0, tiled=True)
         gwg, gwu, gwd = _grads(xc, hdd, NFULL, ff, grads)
 

time: 167 us -> 165 us (0.988)
  waiting for transfers between devices: 2.13 us -> 0.44 us
    pallas_call x1, Pallas kernels: 105 us -> 101 us  [_exchange(): pl.pallas_call(functools.partial(_exchange_kernel, nch, nfull), out_shape...]
    pallas_call x1, Pallas kernels: 18.4 us -> 20.7 us  [_finish(): pl.pallas_call(functools.partial(_finish_kernel, nfull, nrest), out_shape...]
    all_to_all x1, waiting for transfers between devices: 2.11 us -> 0.43 us  [local_step(): got = lax.all_to_all(give, ('tp', 'dp'), 0, 0, tiled=True)]
where the time goes in v5:
time: 165 us
  Pallas kernels  158 us (96%)
  starting transfers between devices  3.96 us (2%)
  other arithmetic  1.69 us (1%)
    pallas_call x1, Pallas kernels, _exchange(): pl.pallas_call(functools.partial(_exchange_kernel, nch, nfull), out_shape...  101 us
    pallas_call x2, Pallas kernels, _grads(): pl.pallas_call(functools.partial(_grads_kernel, base, nch), out_shape=(ja...  36 us
    pallas_call x1, Pallas kernels, _finish(): pl.pallas_call(functools.partial(_finish_kernel, nfull, nrest), out_shape...  20.7 us
  transfers between devices with their start and end apart: 2, of which 1 were waited for; matrix products, arithmetic and copies ran while one was open for 0% of the time, Pallas kernels for 22%

profile of v5, /device:TPU:0, one launch (start us, length us, event | category | flops | bytes accessed | tf_op | source)
XLA Modules:
  0.0 164.8 jit_solution(9619705818318551652)
XLA Ops:
  0.6 101.3 %exchange.1 = (f32[2,128,896]{2,1,0:T(8,128)}, bf16[2,128,896]{2,1,0:T(8,128)(2,1)}, bf16[24,3,128,256]{3,2,1,0:T(8,128)(2,1)}, f32[10,3,32,256]{3,2,1,0:T(8,128...) custom-call(bf16[16,3584]{1,0:T(8,128)(2,1)} %x_ref.1, bf16[16,3584]{1,0:T(8,128)(2,1)} %gy_ref.1, ...), custom_call_target="tpu_custom_call" | custom-call | flops 13035896832 | bytes 50921472 | tf_op jit(solution)/shard_map/exchange/pallas_call | solution.py:305
  101.9 1.7 %collective-permute-start = (f32[10,3,32,256]{3,2,1,0:T(8,128)}, f32[10,3,32,256]{3,2,1,0:T(8,128)}, u32[]{:S(2)}, u32[]{:S(2)}) collective-permute-start(f32[10,3,32,256]{3,2,1,0:T(8,128)} %get-tuple-element.32), channel_id=1, source_target_pairs={{0,2},{1,3},{2,0},{3,1},{4,6},{5,7},{6,4},{7,5}} | collective-permute-start | bytes 2949128 | tf_op jit(solution)/shard_map/ppermute | solution.py:564
  103.6 22.6 %grads.2 = (f32[896,9472]{1,0:T(8,128)}, f32[896,9472]{1,0:T(8,128)}, f32[9472,896]{1,0:T(8,128)}) custom-call(bf16[2,128,896]{2,1,0:T(8,128)(2,1)} %get-tuple-element.24.xc_ref, bf16[24,3,128,256]{3,2,1,0:T(8,128)(2,1)} %get-tuple-element.25.hdd_ref), custom_call_target="tpu_custom_call" | custom-call | flops 4227858432 | bytes 66060288 | tf_op jit(solution)/shard_map/grads/pallas_call | solution.py:540
  126.2 0.0 collective-permute-done.got_ref
  126.2 20.7 %finish.1 = (f32[8,2,16,896]{3,2,1,0:T(8,128)}, bf16[13,3,128,256]{3,2,1,0:T(8,128)(2,1)}) custom-call(f32[2,128,896]{2,1,0:T(8,128)} %get-tuple-element.23.acc_in, f32[13,3,32,256]{3,2,1,0:T(8,128)} %get-tuple-element.30.keep_ref, f32[3,3,32,256]{3,2,1,0:T(8,128)} %get-tuple-element.31.tail_ref, f32[10,3,32,256]{3,2,1,0:T(8,128)} %collective-permute-done.got_ref, ...), custom_call_target="tpu_custom_call" | custom-call | flops 2290089984 | bytes 17891328 | tf_op jit(solution)/shard_map/finish/pallas_call | solution.py:461
  146.9 2.3 %all-to-all-start = ((f32[8,2,16,896]{3,2,1,0:T(8,128)}), f32[8,2,16,896]{3,2,1,0:T(8,128)S(1)}, u32[]{:S(2)}, u32[]{:S(2)}) async-start(f32[8,2,16,896]{3,2,1,0:T(8,128)} %get-tuple-element.33), calls=%async_computation | async-start | bytes 1835008 | tf_op jit(solution)/shard_map/all_to_all | solution.py:568
  149.3 0.0 copy-start
  149.3 13.4 %grads.3 = (f32[896,9472]{1,0:T(8,128)}, f32[896,9472]{1,0:T(8,128)}, f32[9472,896]{1,0:T(8,128)}) custom-call(bf16[2,128,896]{2,1,0:T(8,128)(2,1)} %get-tuple-element.24.xc_ref, bf16[13,3,128,256]{3,2,1,0:T(8,128)(2,1)} %get-tuple-element.34.hdd_ref, ...), custom_call_target="tpu_custom_call", output_to_operand_aliasing={{0}: (2, {}), {1}: (3, {}), {2}: (4, {})} | custom-call | flops 2290089984 | bytes 35782656 | tf_op jit(solution)/shard_map/grads/pallas_call | solution.py:540
  162.7 0.4 all-to-all-done
  163.2 0.0 copy-done
  163.2 1.6 fusion
  (1 shorter events, 0.0 us)
Async XLA Ops:
  101.9 24.2 %collective-permute-start = (f32[10,3,32,256]{3,2,1,0:T(8,128)}, f32[10,3,32,256]{3,2,1,0:T(8,128)}, u32[]{:S(2)}, u32[]{:S(2)}) collective-permute-start(f32[10,3,32,256]{3,2,1,0:T(8,128)} %get-tuple-element.32), channel_id=1, source_target_pairs={{0,2},{1,3},{2,0},{3,1},{4,6},{5,7},{6,4},{7,5}} | collective-permute-start | bytes 2949128 | tf_op jit(solution)/shard_map/ppermute | solution.py:564
  146.9 16.2 %all-to-all-start = ((f32[8,2,16,896]{3,2,1,0:T(8,128)}), f32[8,2,16,896]{3,2,1,0:T(8,128)S(1)}, u32[]{:S(2)}, u32[]{:S(2)}) async-start(f32[8,2,16,896]{3,2,1,0:T(8,128)} %get-tuple-element.33), calls=%async_computation | async-start | bytes 1835008 | tf_op jit(solution)/shard_map/all_to_all | solution.py:568
  149.3 13.9 %copy-start = (bf16[16,3584]{1,0:T(8,128)(2,1)S(1)}, bf16[16,3584]{1,0:T(8,128)(2,1)}, u32[]{:S(2)}) copy-start(bf16[16,3584]{1,0:T(8,128)(2,1)} %x_ref.1) | copy-start | bytes 344068

commit v6 on v5

--- a/solution.py
+++ b/solution.py
@@ -38,11 +38,11 @@
                                         device_id=dev, device_id_type=pl.DeviceIdType.MESH)
 
 
-def _exchange_kernel(nch, nfull, x_ref, gy_ref, wg_ref, wu_ref, wd_ref,
-                     acc, xc_out, hdd_out, give_out, keep_out, got_out,
-                     xc, wgb, wub, wdb, wgb2, wub2, wdb2, part, rdat, sx, rx, hdd, give, keep,
+def _exchange_kernel(nch, nfull, x_in, gy_in, wg_ref, wu_ref, wd_ref,
+                     acc_out, xc_out, hdd_out, give_out, keep_out, got_out,
+                     acc, x_ref, gy_ref, xc, wgb, wub, wdb, wgb2, wub2, wdb2, part, rdat, sx, rx, hdd, give, keep,
                      wsem, wsem2, tsem_s, tsem_r, ds, dr, xs, xr, gs, gr, fs, fr, osem, csem, ksem, absem,
-                     ts, tr):
+                     ts, tr, rsem, asem):
     nrest = nch - nfull
     dp = lax.axis_index("dp")
     tp = lax.axis_index("tp")
@@ -70,6 +70,10 @@
     def rest_w(r):
         return wcopies(nfull + r, r % SLOTS2, (wgb2, wub2, wdb2), wsem2)
 
+    rows = [pltpu.make_async_copy(x_in, x_ref, rsem.at[0]),
+            pltpu.make_async_copy(gy_in, gy_ref, rsem.at[1])]
+    for c in rows:
+        c.start()
     for j in range(AHEAD + 1):
         for c in first_w(j):
             c.start()
@@ -93,6 +97,7 @@
     pos = pl.multiple_of(co * 64 + xi * 32 + tp * 16, 16)
     tok = []
     for k, src in enumerate((x_ref, gy_ref)):
+        rows[k].wait()
         for n, r in enumerate(rel):
             q, pt = peer(r)
             qcols = pl.ds(pl.multiple_of(q * dd, 128), dd)
@@ -265,6 +270,8 @@
 
     cc = pltpu.make_async_copy(xc, xc_out, csem)
     cc.start()
+    ac = pltpu.make_async_copy(acc, acc_out, asem)
+    ac.start()
 
     def finish_full(j, carry):
         x_copy(j).wait_send()
@@ -292,6 +299,7 @@
     for r in range(NTAIL):
         t_copy(r).wait()
     cc.wait()
+    ac.wait()
 
 
 def _exchange(x_loc, gy_loc, wg, wu, wd, nfull):
@@ -299,7 +307,6 @@
     nch = ff // CW
     nrest = nch - nfull
     tok = 128
-    vm = pl.BlockSpec(memory_space=pltpu.VMEM)
     hbm = pl.BlockSpec(memory_space=pl.ANY)
     dma = pltpu.SemaphoreType.DMA
     return pl.pallas_call(
@@ -310,9 +317,12 @@
                    jax.ShapeDtypeStruct((nrest - NTAIL, 3, 32, CW), F32),
                    jax.ShapeDtypeStruct((nrest, 3, 32, CW), F32),
                    jax.ShapeDtypeStruct((NTAIL, 3, 32, CW), F32)),
-        in_specs=[vm, vm, hbm, hbm, hbm],
-        out_specs=(vm, hbm, hbm, hbm, hbm, hbm),
+        in_specs=[hbm] * 5,
+        out_specs=(hbm,) * 6,
         scratch_shapes=[
+            pltpu.VMEM((2, tok, dd), F32),
+            pltpu.VMEM(x_loc.shape, BF16),
+            pltpu.VMEM(gy_loc.shape, BF16),
             pltpu.VMEM((2, tok, dd), BF16),
             pltpu.VMEM((SLOTS, dd, CW), BF16),
             pltpu.VMEM((SLOTS, dd, CW), BF16),
@@ -331,9 +341,10 @@
             dma((nch,)), dma((nch,)), dma((nfull,)), dma((nfull,)),
             dma((nfull,)), dma((nfull,)), dma((nfull,)), dma((nfull,)),
             dma((nfull,)), dma(()), dma((2, nrest)), dma(()), dma((NTAIL,)), dma((NTAIL,)),
+            dma((2,)), dma(()),
         ],
         compiler_params=pltpu.CompilerParams(
-            collective_id=0, has_side_effects=True, vmem_limit_bytes=66 * 1000 * 1000),
+            collective_id=0, has_side_effects=True, vmem_limit_bytes=67_043_328),
         cost_estimate=pl.CostEstimate(flops=12 * tok * dd * ff, bytes_accessed=6 * dd * ff,
                                       transcendentals=0),
         name="exchange",
@@ -341,8 +352,8 @@
 
 
 def _finish_kernel(nfull, nrest, acc_in, keep_ref, tail_ref, got_ref, wg_ref, wu_ref, wd_ref,
-                   give, hdd_out, acc, keep, got, wgb, wub, wdb, hdd,
-                   wsem, isem, asem, gs, gr, fs, fr, osem):
+                   give_out, hdd_out, give, acc, keep, got, wgb, wub, wdb, hdd,
+                   wsem, isem, asem, vsem, gs, gr, fs, fr, osem):
     dp = lax.axis_index("dp")
     xi = dp // 2
     co = dp % 2
@@ -440,6 +451,8 @@
         for q in range(4):
             row = (q % 2) * 64 + (q // 2) * 32 + t * 16
             give[t * 4 + q] = acc[:, row:row + 16, :]
+    vcopy = pltpu.make_async_copy(give, give_out, vsem)
+    vcopy.start()
 
     def finish(r, carry):
         g_copy(r).wait_send()
@@ -448,6 +461,7 @@
         return carry
 
     lax.fori_loop(0, nrest, finish, 0)
+    vcopy.wait()
 
 
 def _finish(acc, keep, tail, got, wg, wu, wd):
@@ -455,7 +469,6 @@
     nrest = keep.shape[0]
     nfull = ff // CW - nrest
     tok = acc.shape[1]
-    vm = pl.BlockSpec(memory_space=pltpu.VMEM)
     hbm = pl.BlockSpec(memory_space=pl.ANY)
     dma = pltpu.SemaphoreType.DMA
     return pl.pallas_call(
@@ -463,8 +476,9 @@
         out_shape=(jax.ShapeDtypeStruct((8, 2, 16, dd), F32),
                    jax.ShapeDtypeStruct((nrest, 3, tok, CW), BF16)),
         in_specs=[hbm] * 7,
-        out_specs=(vm, hbm),
+        out_specs=(hbm, hbm),
         scratch_shapes=[
+            pltpu.VMEM((8, 2, 16, dd), F32),
             pltpu.VMEM((2, tok, dd), F32),
             pltpu.VMEM((nrest, 3, 32, CW), F32),
             pltpu.VMEM((nrest, 3, 32, CW), F32),
@@ -472,7 +486,7 @@
             pltpu.VMEM((nrest, dd, CW), BF16),
             pltpu.VMEM((nrest, CW, dd), BF16),
             pltpu.VMEM((nrest, 3, tok, CW), BF16),
-            dma((3, nrest)), dma((2, nrest)), dma(()), dma((nrest,)), dma((nrest,)), dma((nrest,)), dma((nrest,)),
+            dma((3, nrest)), dma((2, nrest)), dma(()), dma(()), dma((nrest,)), dma((nrest,)), dma((nrest,)), dma((nrest,)),
             dma((nrest,)),
         ],
         compiler_params=pltpu.CompilerParams(

time: 165 us -> 164 us (level)
  transfers between devices with their start and end apart: 2 -> 2, of which waited for: 1 -> 2; matrix products, arithmetic and copies ran while one was open for 0% -> 0% of each run, Pallas kernels for 22% -> 22%
where the time goes in v6:
time: 164 us
  Pallas kernels  157 us (96%)
  starting transfers between devices  2.7 us (2%)
  other arithmetic  1.69 us (1%)
    pallas_call x1, Pallas kernels, _exchange(): pl.pallas_call(functools.partial(_exchange_kernel, nch, nfull), out_shape...  101 us
    pallas_call x2, Pallas kernels, _grads(): pl.pallas_call(functools.partial(_grads_kernel, base, nch), out_shape=(ja...  36 us
    pallas_call x1, Pallas kernels, _finish(): pl.pallas_call(functools.partial(_finish_kernel, nfull, nrest), out_shape...  20.5 us
  transfers between devices with their start and end apart: 2, of which 2 were waited for; matrix products, arithmetic and copies ran while one was open for 0% of the time, Pallas kernels for 22%

profile of v6, /device:TPU:0, one launch (start us, length us, event | category | flops | bytes accessed | tf_op | source)
XLA Modules:
  0.0 163.9 jit_solution(15432943602323329900)
XLA Ops:
  0.6 101.0 %exchange.1 = (f32[2,128,896]{2,1,0:T(8,128)}, bf16[2,128,896]{2,1,0:T(8,128)(2,1)}, bf16[24,3,128,256]{3,2,1,0:T(8,128)(2,1)}, f32[10,3,32,256]{3,2,1,0:T(8,128...) custom-call(bf16[16,3584]{1,0:T(8,128)(2,1)} %x_in.1, bf16[16,3584]{1,0:T(8,128)(2,1)} %gy_in.1, ...), custom_call_target="tpu_custom_call" | custom-call | flops 13035896832 | bytes 50921472 | tf_op jit(solution)/shard_map/exchange/pallas_call | solution.py:312
  101.6 0.4 collective-permute-start
  102.0 22.6 %grads.2 = (f32[896,9472]{1,0:T(8,128)}, f32[896,9472]{1,0:T(8,128)}, f32[9472,896]{1,0:T(8,128)}) custom-call(bf16[2,128,896]{2,1,0:T(8,128)(2,1)} %get-tuple-element.24.xc_ref, bf16[24,3,128,256]{3,2,1,0:T(8,128)(2,1)} %get-tuple-element.25.hdd_ref), custom_call_target="tpu_custom_call" | custom-call | flops 4227858432 | bytes 66060288 | tf_op jit(solution)/shard_map/grads/pallas_call | solution.py:554
  124.6 0.9 collective-permute-done.got_ref
  125.6 20.5 %finish.1 = (f32[8,2,16,896]{3,2,1,0:T(8,128)}, bf16[13,3,128,256]{3,2,1,0:T(8,128)(2,1)}) custom-call(f32[2,128,896]{2,1,0:T(8,128)} %get-tuple-element.23.acc_in, f32[13,3,32,256]{3,2,1,0:T(8,128)} %get-tuple-element.30.keep_ref, f32[3,3,32,256]{3,2,1,0:T(8,128)} %get-tuple-element.31.tail_ref, f32[10,3,32,256]{3,2,1,0:T(8,128)} %collective-permute-done.got_ref, ...), custom_call_target="tpu_custom_call" | custom-call | flops 2290089984 | bytes 17891328 | tf_op jit(solution)/shard_map/finish/pallas_call | solution.py:474
  146.0 2.3 %all-to-all-start = ((f32[8,2,16,896]{3,2,1,0:T(8,128)}), f32[8,2,16,896]{3,2,1,0:T(8,128)S(1)}, u32[]{:S(2)}, u32[]{:S(2)}) async-start(f32[8,2,16,896]{3,2,1,0:T(8,128)} %get-tuple-element.33), calls=%async_computation | async-start | bytes 1835008 | tf_op jit(solution)/shard_map/all_to_all | solution.py:582
  148.4 0.0 copy-start
  148.4 13.4 %grads.3 = (f32[896,9472]{1,0:T(8,128)}, f32[896,9472]{1,0:T(8,128)}, f32[9472,896]{1,0:T(8,128)}) custom-call(bf16[2,128,896]{2,1,0:T(8,128)(2,1)} %get-tuple-element.24.xc_ref, bf16[13,3,128,256]{3,2,1,0:T(8,128)(2,1)} %get-tuple-element.34.hdd_ref, ...), custom_call_target="tpu_custom_call", output_to_operand_aliasing={{0}: (2, {}), {1}: (3, {}), {2}: (4, {})} | custom-call | flops 2290089984 | bytes 35782656 | tf_op jit(solution)/shard_map/grads/pallas_call | solution.py:554
  161.8 0.4 all-to-all-done
  162.3 0.0 copy-done
  162.3 1.6 fusion
  (1 shorter events, 0.0 us)
Async XLA Ops:
  101.6 23.9 %collective-permute-start = (f32[10,3,32,256]{3,2,1,0:T(8,128)}, f32[10,3,32,256]{3,2,1,0:T(8,128)}, u32[]{:S(2)}, u32[]{:S(2)}) collective-permute-start(f32[10,3,32,256]{3,2,1,0:T(8,128)} %get-tuple-element.32), channel_id=1, source_target_pairs={{0,2},{1,3},{2,0},{3,1},{4,6},{5,7},{6,4},{7,5}} | collective-permute-start | bytes 2949128 | tf_op jit(solution)/shard_map/ppermute | solution.py:578
  146.0 16.2 %all-to-all-start = ((f32[8,2,16,896]{3,2,1,0:T(8,128)}), f32[8,2,16,896]{3,2,1,0:T(8,128)S(1)}, u32[]{:S(2)}, u32[]{:S(2)}) async-start(f32[8,2,16,896]{3,2,1,0:T(8,128)} %get-tuple-element.33), calls=%async_computation | async-start | bytes 1835008 | tf_op jit(solution)/shard_map/all_to_all | solution.py:582
  148.4 13.9 %copy-start = (bf16[16,3584]{1,0:T(8,128)(2,1)S(1)}, bf16[16,3584]{1,0:T(8,128)(2,1)}, u32[]{:S(2)}) copy-start(bf16[16,3584]{1,0:T(8,128)(2,1)} %x_in.1) | copy-start | bytes 344068
